TPU v7x, 512 devices: a whole 4x4x16 slice. The times are simulated.
512 devices in a mesh: grp: 16 (over z), dev: 32 (over x, y, core).
Axes of the slice: x: 4, y: 4, z: 16, core: 2. Of those that a mesh axis runs over, the one named last changes fastest.
Arguments:
- root_solution: bfloat16 [4096, 256], P(('grp', 'dev')), may hold values from -6 to 6
- sep_rhs: bfloat16 [65536, 256], P(('grp', 'dev')), may hold values from -6 to 6
- sep_update: bfloat16 [65536, 512], P(('grp', 'dev')), may hold values from -0.25 to 0.25
- sep_rows: int32 [16, 512], P('grp'), may hold values from 0 to 4095
- sep_inv_cols: bfloat16 [65536, 4096], P(('grp', 'dev')), may hold values from -0.375 to 0.375
- leaf_rhs: bfloat16 [524288, 256], P(('grp', 'dev')), may hold values from -6 to 6
- leaf_update: bfloat16 [524288, 256], P(('grp', 'dev')), may hold values from -0.375 to 0.375
- leaf_rows: int32 [512, 256], P(('grp', 'dev')), may hold values from 0 to 8191
- leaf_cols: int32 [512], P(('grp', 'dev')), may hold values from 512 to 1024, as said below
- leaf_inv: bfloat16 [524288, 1024], P(('grp', 'dev')), may hold values from -0.1875 to 0.1875
Outputs:
- sep_solution: bfloat16 [65536, 256], P(('grp', 'dev'))
- leaf_solution: bfloat16 [524288, 256], P(('grp', 'dev'))
Inputs may be any that keep to these rules, and one draw needn't show every extreme that they name: `leaf_cols`: some front has exactly 1024 live columns and some exactly 512.
All inputs are finite; a program needn't handle non-finite values.
Results may differ from a plain program's by a relative error of at most 0.0056.
Values may be sent and summed in bfloat16 or wider, within the bound.
No kernel may reach another device: no remote copies, remote signals or barrier semaphores. Data moves between devices by JAX's collectives and lax.ppermute only.
A program may use at most 64 MiB of HBM per device.

v0:
```python
import jax
import jax.numpy as jnp
from jax import lax
from jax.sharding import Mesh
from jax.sharding import PartitionSpec as P

GRP_DEV = ("grp", "dev_0", "dev_1", "dev_2")
DEV = ("dev_0", "dev_1", "dev_2")


def from_everyone(shard, axis):
    copies = jnp.broadcast_to(shard, (lax.axis_size(axis), *shard.shape))
    return lax.all_to_all(copies, axis, split_axis=0, concat_axis=0, tiled=True)


def joined_along(blocks, dim):
    blocks = jnp.moveaxis(blocks, 0, dim)
    dims = blocks.shape
    return blocks.reshape(*dims[:dim], dims[dim] * dims[dim + 1], *dims[dim + 2 :])


def whole_of(shard, axes, dim):
    far, near = axes
    blocks = from_everyone(from_everyone(shard, far), near)
    return joined_along(blocks.swapaxes(0, 1).reshape(-1, *shard.shape), dim)


def filled_up(lines, size):
    spare = -len(lines) % size
    return jnp.pad(lines, [(0, spare)] + [(0, 0)] * (lines.ndim - 1))


def split_up(shard, dim, size):
    dims = shard.shape
    blocks = shard.reshape(*dims[:dim], size, dims[dim] // size, *dims[dim + 1 :])
    return jnp.moveaxis(blocks, dim, 0)


def sent_and_summed(shard, axis, dim):
    blocks = split_up(shard, dim, lax.axis_size(axis))
    arrived = lax.all_to_all(blocks, axis, split_axis=0, concat_axis=0, tiled=True)
    return arrived.sum(axis=0)


def sum_in_two_steps(shard, axes, dim):
    far, near = axes
    own = sent_and_summed(split_up(shard, dim, lax.axis_size(far)), near, dim + 1)
    return jnp.sum(lax.all_to_all(own, far, 0, 0, tiled=True), axis=0)


def nested_sum(shard, axes):
    lines = shard.reshape(-1, shard.shape[-1])
    padded = filled_up(lines, lax.axis_size(axes[0]) * lax.axis_size(axes[1]))
    whole = whole_of(sum_in_two_steps(padded, axes, 0), axes, 0)
    return lax.slice_in_dim(whole, 0, len(lines)).reshape(shard.shape)


def on_device(
    root_solution,
    sep_rhs,
    sep_update,
    sep_rows,
    sep_inv_cols,
    leaf_rhs,
    leaf_update,
    leaf_rows,
    leaf_cols,
    leaf_inv,
):
    tile_rows = sep_rhs.shape[0]
    root_all = whole_of(root_solution, (("grp", "dev_0"), ("dev_1", "dev_2")), 0)
    picked = jnp.take(root_all, sep_rows[0], axis=0)
    sep_residual = (
        sep_rhs.astype(jnp.float32)
        - jnp.dot(sep_update, picked, preferred_element_type=jnp.float32)
    ).astype(jnp.bfloat16)
    contract = (((0,), (0,)), ((), ()))
    partial_value = lax.dot_general(
        sep_inv_cols, sep_residual, contract, preferred_element_type=jnp.float32
    )
    sep_full = nested_sum(partial_value, (("dev_0", "dev_1"), "dev_2")).astype(jnp.bfloat16)
    own_rows = lax.dynamic_slice_in_dim(sep_full, lax.axis_index(DEV) * tile_rows, tile_rows, 0)
    ancestors = jnp.concatenate([sep_full, root_all], axis=0)
    gathered = jnp.take(ancestors, leaf_rows[0], axis=0)
    padded = leaf_rhs.shape[0]
    live_rows = (jnp.arange(padded, dtype=jnp.int32) < leaf_cols[0])[:, None]
    leaf_residual = leaf_rhs.astype(jnp.float32) - jnp.dot(
        leaf_update, gathered, preferred_element_type=jnp.float32
    )
    leaf_residual = jnp.where(live_rows, leaf_residual, jnp.float32(0.0)).astype(jnp.bfloat16)
    solved = jnp.dot(leaf_inv, leaf_residual, preferred_element_type=jnp.float32)
    leaf_out = jnp.where(live_rows, solved, jnp.float32(0.0)).astype(jnp.bfloat16)
    return (own_rows, leaf_out)


def solution(mesh):
    finer = Mesh(
        mesh.devices.reshape(mesh.shape["grp"], 4, 4, 2), ("grp", "dev_0", "dev_1", "dev_2")
    )
    in_specs = (
        P(GRP_DEV, None),
        P(GRP_DEV, None),
        P(GRP_DEV, None),
        P("grp", None),
        P(GRP_DEV, None),
        P(GRP_DEV, None),
        P(GRP_DEV, None),
        P(GRP_DEV, None),
        P(GRP_DEV),
        P(GRP_DEV, None),
    )
    out_specs = (P(GRP_DEV, None), P(GRP_DEV, None))
    return jax.shard_map(
        on_device, mesh=finer, in_specs=in_specs, out_specs=out_specs, check_vma=False
    )
```

profile of v0, /device:TPU:1, one launch (start us, length us, event | category | flops | bytes accessed | tf_op | source)
XLA Modules:
  0.0 183.2 jit_solution(6919008168195809004)
XLA Ops:
  1.5 38.4 %all_to_all.30 = bf16[64,8,256]{2,1,0:T(8,128)(2,1)S(1)} all-to-all(bf16[64,8,256]{2,1,0:T(8,128)(2,1)S(1)} %broadcast_in_dim.54), channel_id=1, replica_groups=mesh['grp'=16,'dev_0'=4,'dev_1'=4,'dev_2'=2] {'grp','dev_0'}, dimensions={0} | all-to-all | bytes 524288 | tf_op jit(solution)/shard_map/all_to_all | solution.py:13
  39.9 1.4 broadcast_in_dim.55
  41.3 8.5 %all-to-all-start.1 = ((bf16[8,64,8,256]{3,2,1,0:T(8,128)(2,1)}), bf16[8,64,8,256]{3,2,1,0:T(8,128)(2,1)}, u32[]{:S(2)}, u32[]{:S(2)}) async-start(bf16[8,64,8,256]{3,2,1,0:T(8,128)(2,1)} %broadcast_in_dim.55), calls=%async_computation.1 | async-start | bytes 4194304 | tf_op jit(solution)/shard_map/all_to_all | solution.py:13
  50.0 26.1 %all-to-all-done.1 = bf16[8,64,8,256]{3,2,1,0:T(8,128)(2,1)} async-done(((bf16[8,64,8,256]{3,2,1,0:T(8,128)(2,1)}), bf16[8,64,8,256]{3,2,1,0:T(8,128)(2,1)}, u32[]{:S(2)}, u32[]{:S(2)}) %all-to-all-start.1) | async-done | bytes 2097184 | tf_op jit(solution)/shard_map/all_to_all | solution.py:13
  76.1 3.2 %copy.22 = bf16[64,8,8,256]{3,2,1,0:T(8,128)(2,1)} copy(bf16[64,8,8,256]{3,2,0,1:T(8,128)(2,1)} %bitcast.1) | data formatting | bytes 4194304 | tf_op jit(solution)/shard_map/transpose | solution.py:25
  79.4 3.5 %gather_fusion = bf16[512,256]{1,0:T(8,128)(2,1)S(1)} fusion(bf16[4096,256]{1,0:T(8,128)(2,1)} %bitcast.47, s32[1024]{0:T(1024)S(1)} %pad_clamp_fusion.1), kind=kCustom, calls=%fused_computation | custom fusion | bytes 526336 | tf_op jit(solution)/shard_map/jit(_take)/gather | solution.py:72
  82.9 3.9 %convolution_bitcast_fusion = f32[4096,256]{0,1:T(8,128)} fusion(bf16[128,4096]{1,0:T(8,128)(2,1)S(1)} %copy-done.2, bf16[128,512]{1,0:T(8,128)(2,1)} %param.12, bf16[512,256]{1,0:T(8,128)(2,1)S(1)} %gather_fusion, pred[512]{0:T(512)(128)(4,1)S(1)} %compare_and_fusion.1, bf16[128,256]{0,1:T(8,128)(2,1)S(1)} %copy.21), kind=kOutput, calls=%fused_computation.2 | convolution fusion | flops 302219264 | bytes 5702144 | tf_op jit(solution)/shard_map/dot_general | solution.py:78
  86.8 6.6 %reshape_reshape.8 = f32[16,2,128,256]{2,1,0,3:T(2,128)} reshape(f32[4096,256]{0,1:T(8,128)} %convolution_bitcast_fusion) | data formatting | bytes 8388608 | tf_op jit(solution)/shard_map/reshape;reshape | solution.py:35
  93.4 2.5 %copy.34 = f32[16,2,128,256]{2,0,3,1:T(8,128)S(1)} copy(f32[16,2,128,256]{2,1,0,3:T(2,128)} %reshape_reshape.8) | data formatting | bytes 8388608 | tf_op jit(solution)/shard_map/reshape;reshape | solution.py:35
  96.0 8.8 %all_to_all.31 = f32[2,16,128,256]{2,1,3,0:T(8,128)} all-to-all(f32[2,16,128,256]{2,1,3,0:T(8,128)S(1)} %bitcast.49), channel_id=1, replica_groups=mesh['grp'=16,'dev_0'=4,'dev_1'=4,'dev_2'=2] {'dev_2'}, dimensions={0} | all-to-all | bytes 8388608 | tf_op jit(solution)/shard_map/all_to_all | solution.py:41
  104.7 4.0 %reduce_sum.18 = f32[16,128,256]{1,0,2:T(8,128)} reduce(f32[2,16,128,256]{2,1,3,0:T(8,128)} %all_to_all.31, f32[]{:T(128)} %constant.27.clone.1), dimensions={0}, to_apply=%region_0.1 | reduce | flops 524288 | bytes 6291460 | tf_op jit(solution)/shard_map/reduce_sum | solution.py:42
  108.8 2.3 %copy.25 = f32[16,128,256]{1,2,0:T(8,128)S(1)} copy(f32[16,128,256]{1,0,2:T(8,128)} %reduce_sum.18) | data formatting | bytes 4194304 | tf_op jit(solution)/shard_map/reduce_sum | solution.py:42
  111.0 30.9 %all_to_all.32 = f32[16,128,256]{1,2,0:T(8,128)} all-to-all(f32[16,128,256]{1,2,0:T(8,128)S(1)} %copy.25), channel_id=1, replica_groups=mesh['grp'=16,'dev_0'=4,'dev_1'=4,'dev_2'=2] {'dev_0','dev_1'}, dimensions={0} | all-to-all | bytes 4194304 | tf_op jit(solution)/shard_map/all_to_all | solution.py:48
  142.0 1.7 reduce_sum.19
  143.8 1.1 broadcast_in_dim.57
  144.9 3.7 %all-to-all-start.4 = ((bf16[16,128,256]{2,1,0:T(8,128)(2,1)}), bf16[16,128,256]{2,1,0:T(8,128)(2,1)S(1)}, u32[]{:S(2)}, u32[]{:S(2)}) async-start(bf16[16,128,256]{2,1,0:T(8,128)(2,1)} %broadcast_in_dim.57), calls=%async_computation.4 | async-start | bytes 2097152 | tf_op jit(solution)/shard_map/all_to_all | solution.py:13
  148.6 2.0 %copy.29 = bf16[1024,256]{0,1:T(8,128)(2,1)} copy(bf16[1024,256]{1,0:T(8,128)(2,1)} %param.15) | data formatting | bytes 1048576 | tf_op args[5]
  151.4 12.3 %all-to-all-done.4 = bf16[16,128,256]{2,1,0:T(8,128)(2,1)S(1)} async-done(((bf16[16,128,256]{2,1,0:T(8,128)(2,1)}), bf16[16,128,256]{2,1,0:T(8,128)(2,1)S(1)}, u32[]{:S(2)}, u32[]{:S(2)}) %all-to-all-start.4) | async-done | bytes 1048608 | tf_op jit(solution)/shard_map/all_to_all | solution.py:13
  164.0 8.1 %all_to_all.33 = bf16[2,16,128,256]{3,2,1,0:T(8,128)(2,1)S(1)} all-to-all(bf16[2,16,128,256]{3,2,1,0:T(8,128)(2,1)S(1)} %broadcast_in_dim.58), channel_id=1, replica_groups=mesh['grp'=16,'dev_0'=4,'dev_1'=4,'dev_2'=2] {'dev_2'}, dimensions={0} | all-to-all | bytes 4194304 | tf_op jit(solution)/shard_map/all_to_all | solution.py:13
  172.2 1.4 copy-done.1
  173.6 2.2 %pad_maximum_fusion = bf16[8192,256]{1,0:T(8,128)(2,1)} fusion(bf16[4096,256]{1,0:T(8,128)(2,1)S(1)} %bitcast.48, bf16[4096,256]{1,0:T(8,128)(2,1)S(1)} %bitcast.50), kind=kLoop, calls=%fused_computation.3 | loop fusion | flops 8388608 | bytes 8388608 | tf_op jit(solution)/shard_map/concatenate | solution.py:83
  176.4 3.7 %gather_fusion.1 = bf16[256,256]{1,0:T(8,128)(2,1)S(1)} fusion(bf16[8192,256]{1,0:T(8,128)(2,1)} %pad_maximum_fusion, s32[1024]{0:T(1024)S(1)} %pad_clamp_fusion), kind=kCustom, calls=%fused_computation.1 | custom fusion | bytes 263168 | tf_op jit(solution)/shard_map/jit(_take)/gather | solution.py:84
  180.2 2.0 %fusion.4 = bf16[1024,256]{0,1:T(8,128)(2,1)S(1)} fusion(bf16[1024,1024]{1,0:T(8,128)(2,1)S(1)} %copy-done, bf16[1024,256]{1,0:T(8,128)(2,1)} %param.16, bf16[1024,256]{0,1:T(8,128)(2,1)S(1)} %copy-done.3, pred[1024]{0:T(1024)(128)(4,1)S(1)} %iota_compare_fusion, bf16[256,256]{1,0:T(8,128)(2,1)S(1)} %gather_fusion.1, pred[256]{0:T(512)(128)(4,1)S(1)} %compare_and_fusion), kind=kOutput, calls=%fused_computation.12 | convolution fusion | flops 672727040 | bytes 3802368 | tf_op jit(solution)/shard_map/dot_general | solution.py:91
  182.2 1.0 copy.30
  (26 shorter events, 2.1 us)
Async XLA Ops:
  0.6 179.5 %copy-start = (bf16[1024,1024]{1,0:T(8,128)(2,1)S(1)}, bf16[1024,1024]{1,0:T(8,128)(2,1)}, u32[]{:S(2)}) copy-start(bf16[1024,1024]{1,0:T(8,128)(2,1)} %param.19) | copy-start | bytes 6291460
  41.3 8.5 %copy-start.4 = (bf16[128,256]{1,0:T(8,128)(2,1)S(1)}, bf16[128,256]{1,0:T(8,128)(2,1)}, u32[]{:S(2)}) copy-start(bf16[128,256]{1,0:T(8,128)(2,1)} %param.11) | copy-start | bytes 196612
  41.3 8.6 %copy-start.5 = (s32[1,512]{1,0:T(1,128)S(1)}, s32[1,512]{1,0:T(1,128)}, u32[]{:S(2)}) copy-start(s32[1,512]{1,0:T(1,128)} %param.13) | copy-start | bytes 6148
  41.3 34.8 %all-to-all-start.1 = ((bf16[8,64,8,256]{3,2,1,0:T(8,128)(2,1)}), bf16[8,64,8,256]{3,2,1,0:T(8,128)(2,1)}, u32[]{:S(2)}, u32[]{:S(2)}) async-start(bf16[8,64,8,256]{3,2,1,0:T(8,128)(2,1)} %broadcast_in_dim.55), calls=%async_computation.1 | async-start | bytes 4194304 | tf_op jit(solution)/shard_map/all_to_all | solution.py:13
  79.4 3.5 %copy-start.2 = (bf16[128,4096]{1,0:T(8,128)(2,1)S(1)}, bf16[128,4096]{1,0:T(8,128)(2,1)}, u32[]{:S(2)}) copy-start(bf16[128,4096]{1,0:T(8,128)(2,1)} %param.14) | copy-start | bytes 3145732
  143.8 7.5 %copy-start.6 = (s32[1,256]{1,0:T(1,128)S(1)}, s32[1,256]{1,0:T(1,128)}, u32[]{:S(2)}) copy-start(s32[1,256]{1,0:T(1,128)} %param.17) | copy-start | bytes 3076
  144.9 18.8 %all-to-all-start.4 = ((bf16[16,128,256]{2,1,0:T(8,128)(2,1)}), bf16[16,128,256]{2,1,0:T(8,128)(2,1)S(1)}, u32[]{:S(2)}, u32[]{:S(2)}) async-start(bf16[16,128,256]{2,1,0:T(8,128)(2,1)} %broadcast_in_dim.57), calls=%async_computation.4 | async-start | bytes 2097152 | tf_op jit(solution)/shard_map/all_to_all | solution.py:13
  172.0 1.6 copy-start.1
  173.6 6.5 %copy-start.3 = (bf16[1024,256]{0,1:T(8,128)(2,1)S(1)}, bf16[1024,256]{0,1:T(8,128)(2,1)}, u32[]{:S(2)}) copy-start(bf16[1024,256]{0,1:T(8,128)(2,1)} %copy.29) | copy-start | bytes 1572868
where the time goes:
time: 184 us; the launch traced here: 183 us
  blocking collectives  86.1 us (47%)
  waiting for transfers between devices  38.5 us (21%)
  local copies, waits for them, and re-layouts  30.9 us (17%)
  starting transfers between devices  12.2 us (7%)
  other arithmetic  7.98 us (4%)
  matrix products  5.97 us (3%)
    all_to_all x2, blocking collectives, from_everyone(): return lax.all_to_all(copies, axis, split_axis=0, concat_axis=0, tiled=True)  46.4 us
    all_to_all x2, waiting for transfers between devices, from_everyone(): return lax.all_to_all(copies, axis, split_axis=0, concat_axis=0, tiled=True)  38.5 us
    all_to_all x1, blocking collectives, sum_in_two_steps(): return jnp.sum(lax.all_to_all(own, far, 0, 0, tiled=True), axis=0)  30.9 us
    all_to_all x2, starting transfers between devices, from_everyone(): return lax.all_to_all(copies, axis, split_axis=0, concat_axis=0, tiled=True)  12.2 us
    another operation x2, local copies, waits for them, and re-layouts, split_up(): shard.reshape(*dims[:dim], size, dims[dim] // size, *dims[dim + 1:])  9.12 us
    all_to_all x1, blocking collectives, sent_and_summed(): lax.all_to_all(blocks, axis, split_axis=0, concat_axis=0, tiled=True)  8.76 us
    unnamed x17, local copies, waits for them, and re-layouts  4.64 us
    reduce_sum x1, other arithmetic, sent_and_summed(): return arrived.sum(axis=0)  4.04 us
  transfers between devices with their start and end apart: 2, of which 2 were waited for; matrix products, arithmetic and copies ran while one was open for 1% of the time, Pallas kernels for 0%

commit v1 on v0

v1 whole, which is shorter than its diff:
```python
import jax
import jax.numpy as jnp
from jax import lax
from jax.experimental import pallas as pl
from jax.experimental.pallas import tpu as pltpu
from jax.sharding import Mesh
from jax.sharding import PartitionSpec as P

ALL = ("grp", "dev_0", "dev_1", "dev_2")
XY = ("dev_0", "dev_1")
CORE = "dev_2"
BF16, F32, I32 = jnp.bfloat16, jnp.float32, jnp.int32
MIB = 1 << 20


def to_all(blocks, axes):
    return lax.all_to_all(blocks, axes, 0, 0, tiled=True)


def swapped(value):
    return lax.ppermute(value, CORE, [(0, 1), (1, 0)])


def dot(a, b, dims=((1,), (0,))):
    return lax.dot_general(a, b, (dims, ((), ())), preferred_element_type=F32)


def picked(places, table):
    lines = lax.broadcasted_iota(I32, (places.shape[0], table.shape[0]), 1)
    chosen = jnp.where(lines == places, F32(1.0), F32(0.0)).astype(BF16)
    return dot(chosen, table)


def kernel_call(body, outs, flops, n_bytes, name, in_smem=()):
    def call(*args):
        specs = [
            pl.BlockSpec(memory_space=pltpu.SMEM if i in in_smem else pltpu.VMEM)
            for i in range(len(args))
        ]
        return pl.pallas_call(
            body,
            out_shape=outs,
            in_specs=specs,
            out_specs=jax.tree.map(lambda _: pl.BlockSpec(memory_space=pltpu.VMEM), outs),
            cost_estimate=pl.CostEstimate(flops=flops, bytes_accessed=n_bytes, transcendentals=0),
            compiler_params=pltpu.CompilerParams(vmem_limit_bytes=24 * MIB),
            name=name,
        )(*args)

    return call


def pick_body(places, table, out):
    out[...] = picked(places[...], table[...]).astype(BF16)


def residual_body(half, other, rhs, update, out):
    rows = half[...] + other[...]
    value = (rhs[...].astype(F32) - dot(update[...], rows)).astype(BF16)
    for i in range(out.shape[0]):
        out[i] = value


def partial_body(core, inverse, residual, own, other):
    both = dot(inverse[...], residual[...], ((0,), (0,)))
    half = both.shape[0] // 2
    low, high = both[:half], both[half:]
    first = core[0] == 0
    own[...] = jnp.where(first, low, high)
    other[...] = jnp.where(first, high, low)


def solution_body(own, other, out, copies):
    value = (own[...] + other[...]).astype(BF16)
    out[...] = value
    for i in range(copies.shape[0]):
        copies[i] = value


def ancestors_body(places, table, from_root, own, other):
    both = (picked(places[...], table[...]) + from_root[...].astype(F32)).astype(BF16)
    half = both.shape[0] // 2
    own[...] = both[:half]
    other[...] = both[half:]


def leaf_body(cols, own, other, rhs, update, inverse, out):
    rows = own[...] + other[...]
    live = lax.broadcasted_iota(I32, out.shape, 0) < cols[0]
    residual = rhs[...].astype(F32) - dot(update[...], rows)
    residual = jnp.where(live, residual, F32(0.0)).astype(BF16)
    solved = dot(inverse[...], residual)
    out[...] = jnp.where(live, solved, F32(0.0)).astype(BF16)


def on_device(
    root_solution,
    sep_rhs,
    sep_update,
    sep_rows,
    sep_inv_cols,
    leaf_rhs,
    leaf_update,
    leaf_rows,
    leaf_cols,
    leaf_inv,
):
    groups = lax.axis_size("grp")
    chips = lax.axis_size(XY)
    cores = lax.axis_size(CORE)
    devices = chips * cores
    core = lax.axis_index(CORE)
    own_root, nrhs = root_solution.shape
    own_sep, sep = sep_inv_cols.shape
    root = own_root * groups * devices
    held = sep // cores
    held_root = root // cores
    n_rows = leaf_rows.shape[1]

    def root_places(rows):
        device = rows // own_root % devices
        place = (device // cores * groups + rows // (own_root * devices)) * own_root + rows % own_root
        return jnp.where(device % cores == core, place, -1)

    def sep_places(rows):
        device = rows // own_sep
        return jnp.where(device % cores == core, device // cores * own_sep + rows % own_sep, -1)

    from_groups = to_all(jnp.broadcast_to(root_solution, (groups, own_root, nrhs)), "grp")
    own_lines = from_groups.reshape(groups * own_root, nrhs)
    root_held = to_all(jnp.broadcast_to(own_lines, (chips, *own_lines.shape)), XY)
    root_held = root_held.reshape(held_root, nrhs)

    blocks = sep_inv_cols.reshape(own_sep, chips, sep // chips).transpose(1, 0, 2)
    inverse = to_all(blocks, XY).reshape(held, sep // chips)

    both_rows = jnp.concatenate([leaf_rows[0], swapped(leaf_rows)[0]])
    at_root = jnp.where(both_rows >= sep, root_places(both_rows - sep), -1)[:, None]
    at_sep = jnp.where(both_rows < sep, sep_places(both_rows), -1)[:, None]

    rows_shape = jax.ShapeDtypeStruct((sep_rows.shape[1], nrhs), BF16)
    half = kernel_call(pick_body, rows_shape, 2 * rows_shape.size * held_root, 2 * MIB, "pick_sep")(
        root_places(sep_rows[0])[:, None], root_held
    )
    leaf_root = kernel_call(
        pick_body,
        jax.ShapeDtypeStruct((2 * n_rows, nrhs), BF16),
        4 * n_rows * nrhs * held_root,
        2 * MIB,
        "pick_leaf",
    )(at_root, root_held)

    copies_shape = jax.ShapeDtypeStruct((chips, own_sep, nrhs), BF16)
    part_shape = jax.ShapeDtypeStruct((own_sep, nrhs), F32)
    residual = kernel_call(residual_body, copies_shape, 2 * sep_update.size * nrhs, 2 * MIB, "residual")(
        half, swapped(half), sep_rhs, sep_update
    )
    residual = to_all(residual, XY).reshape(held, nrhs)
    own, other = kernel_call(
        partial_body, (part_shape, part_shape), 2 * inverse.size * nrhs, 3 * MIB, "partial", (0,)
    )(core.astype(I32)[None], inverse, residual)
    sep_out, copies = kernel_call(
        solution_body,
        (jax.ShapeDtypeStruct((own_sep, nrhs), BF16), copies_shape),
        part_shape.size,
        2 * MIB,
        "sum",
    )(own, swapped(other))
    sep_held = to_all(copies, XY).reshape(held, nrhs)

    half_shape = jax.ShapeDtypeStruct((n_rows, nrhs), BF16)
    own_rows, other_rows = kernel_call(
        ancestors_body, (half_shape, half_shape), 4 * n_rows * nrhs * held, 2 * MIB, "ancestors"
    )(at_sep, sep_held, leaf_root)
    leaf_out = kernel_call(
        leaf_body,
        jax.ShapeDtypeStruct(leaf_rhs.shape, BF16),
        2 * nrhs * (leaf_inv.size + leaf_update.size),
        4 * MIB,
        "leaf",
        (0,),
    )(leaf_cols, own_rows, swapped(other_rows), leaf_rhs, leaf_update, leaf_inv)
    return (sep_out, leaf_out)


def solution(mesh):
    finer = Mesh(mesh.devices.reshape(mesh.shape["grp"], 4, 4, 2), ALL)
    split = P(ALL, None)
    in_specs = (split, split, split, P("grp", None), split, split, split, split, P(ALL), split)
    return jax.shard_map(
        on_device, mesh=finer, in_specs=in_specs, out_specs=(split, split), check_vma=False
    )
```

time: 184 us -> 131 us (0.71)
  blocking collectives: 86.1 us -> 46.8 us
  local copies, waits for them, and re-layouts: 30.9 us -> 7.38 us
  starting transfers between devices: 12.2 us -> 31.5 us
  Pallas kernels: 0 us -> 7.2 us
  other arithmetic: 7.98 us -> 1.94 us
  matrix products: 5.97 us -> 0 us
  waiting for transfers between devices: 38.5 us -> 34.2 us
    all_to_all x4 -> x2, blocking collectives: 86.1 us -> 46.8 us  [to_all(): return lax.all_to_all(blocks, axes, 0, 0, tiled=True)]
    ppermute x0 -> x4, starting transfers between devices: none -> 15.6 us  [swapped(): return lax.ppermute(value, CORE, [(0, 1), (1, 0)])]
    another operation x2 -> x0, local copies, waits for them, and re-layouts: 9.12 us -> none  [split_up(): shard.reshape(*dims[:dim], size, dims[dim] // size, *dims[dim + 1:])]
    all_to_all x2 -> x3, waiting for transfers between devices: 38.5 us -> 31 us  [to_all(): return lax.all_to_all(blocks, axes, 0, 0, tiled=True)]
    gather x2 -> x0, local copies, waits for them, and re-layouts: 7.2 us -> none  [the longest x1 3.69 us: on_device(): gathered = jnp.take(ancestors, leaf_rows[0], axis=0)]
    pallas_call x0 -> x7, Pallas kernels: none -> 7.2 us  [call(): pl.pallas_call(body, out_shape=outs, in_specs=specs, out_specs=jax.tree.m...]
    dot_general x2 -> x0, matrix products: 5.97 us -> none  [the longest x1 3.94 us: on_device(): lax.dot_general(sep_inv_cols, sep_residual, contract, preferred_element_t...]
    reduce_sum x2 -> x0, other arithmetic: 5.73 us -> none  [the longest x1 4.04 us: sent_and_summed(): return arrived.sum(axis=0)]
  transfers between devices with their start and end apart: 2 -> 7, of which waited for: 2 -> 7; matrix products, arithmetic and copies ran while one was open for 1% -> 3% of each run, Pallas kernels for 0% -> 1%
where the time goes in v1:
time: 131 us
  blocking collectives  46.8 us (36%)
  waiting for transfers between devices  34.2 us (26%)
  starting transfers between devices  31.5 us (24%)
  local copies, waits for them, and re-layouts  7.38 us (6%)
  Pallas kernels  7.2 us (5%)
  other arithmetic  1.94 us (1%)
  between operations  1.48 us (1%)
    all_to_all x2, blocking collectives, to_all(): return lax.all_to_all(blocks, axes, 0, 0, tiled=True)  46.8 us
    all_to_all x3, waiting for transfers between devices, to_all(): return lax.all_to_all(blocks, axes, 0, 0, tiled=True)  31 us
    all_to_all x3, starting transfers between devices, to_all(): return lax.all_to_all(blocks, axes, 0, 0, tiled=True)  16 us
    ppermute x4, starting transfers between devices, swapped(): return lax.ppermute(value, CORE, [(0, 1), (1, 0)])  15.6 us
    pallas_call x7, Pallas kernels, call(): pl.pallas_call(body, out_shape=outs, in_specs=specs, out_specs=jax.tree.m...  7.2 us
    unnamed x20, local copies, waits for them, and re-layouts  3.76 us
    ppermute x4, waiting for transfers between devices, swapped(): return lax.ppermute(value, CORE, [(0, 1), (1, 0)])  3.22 us
  transfers between devices with their start and end apart: 7, of which 7 were waited for; matrix products, arithmetic and copies ran while one was open for 3% of the time, Pallas kernels for 1%

profile of v1, /device:TPU:1, one launch (start us, length us, event | category | flops | bytes accessed | tf_op | source)
XLA Modules:
  0.0 130.5 jit_solution(16161327750207331250)
XLA Ops:
  1.4 27.1 %all_to_all.25 = bf16[16,8,256]{2,1,0:T(8,128)(2,1)S(1)} all-to-all(bf16[16,8,256]{2,1,0:T(8,128)(2,1)S(1)} %broadcast_in_dim.19), channel_id=1, replica_groups=mesh['grp'=16,'dev_0'=4,'dev_1'=4,'dev_2'=2] {'grp'}, dimensions={0} | all-to-all | bytes 131072 | tf_op jit(solution)/shard_map/all_to_all | solution.py:17
  28.5 1.1 broadcast_in_dim.20
  29.6 6.8 %all-to-all-start.2 = ((bf16[16,128,256]{2,1,0:T(8,128)(2,1)}), bf16[16,128,256]{2,1,0:T(8,128)(2,1)S(1)}, u32[]{:S(2)}, u32[]{:S(2)}) async-start(bf16[16,128,256]{2,1,0:T(8,128)(2,1)} %broadcast_in_dim.20), calls=%async_computation.2 | async-start | bytes 2097152 | tf_op jit(solution)/shard_map/all_to_all | solution.py:17
  36.4 1.1 copy.48
  37.5 13.5 %all-to-all-done.2 = bf16[16,128,256]{2,1,0:T(8,128)(2,1)S(1)} async-done(((bf16[16,128,256]{2,1,0:T(8,128)(2,1)}), bf16[16,128,256]{2,1,0:T(8,128)(2,1)S(1)}, u32[]{:S(2)}, u32[]{:S(2)}) %all-to-all-start.2) | async-done | bytes 1048608 | tf_op jit(solution)/shard_map/all_to_all | solution.py:17
  51.0 4.9 %all-to-all-start = ((bf16[16,128,256]{2,1,0:T(8,128)(2,1)}), bf16[16,128,256]{2,1,0:T(8,128)(2,1)S(1)}, u32[]{:S(2)}, u32[]{:S(2)}) async-start(bf16[16,128,256]{2,1,0:T(8,128)(2,1)} %bitcast.15), calls=%async_computation | async-start | bytes 2097152 | tf_op jit(solution)/shard_map/all_to_all | solution.py:17
  57.5 4.2 %collective-permute-start = (bf16[512,256]{1,0:T(8,128)(2,1)S(1)}, bf16[512,256]{1,0:T(8,128)(2,1)S(1)}, u32[]{:S(2)}, u32[]{:S(2)}) collective-permute-start(bf16[512,256]{1,0:T(8,128)(2,1)S(1)} %pick_sep.1.half), channel_id=1, source_target_pairs={{0,1},{1,0},{2,3},{3,2},{4,5},{5,4},{6,7},{7,6},{8,9},{9,8},{10,11... | collective-permute-start | bytes 786440 | tf_op jit(solution)/shard_map/ppermute | solution.py:21
  61.7 1.1 collective-permute-done.other
  63.1 7.4 %all-to-all-done = bf16[16,128,256]{2,1,0:T(8,128)(2,1)S(1)} async-done(((bf16[16,128,256]{2,1,0:T(8,128)(2,1)}), bf16[16,128,256]{2,1,0:T(8,128)(2,1)S(1)}, u32[]{:S(2)}, u32[]{:S(2)}) %all-to-all-start) | async-done | bytes 1048608 | tf_op jit(solution)/shard_map/all_to_all | solution.py:17
  70.5 19.7 %all_to_all.26 = bf16[16,128,256]{2,1,0:T(8,128)(2,1)S(1)} all-to-all(bf16[16,128,256]{2,1,0:T(8,128)(2,1)S(1)} %residual.1), channel_id=1, replica_groups=mesh['grp'=16,'dev_0'=4,'dev_1'=4,'dev_2'=2] {'dev_0','dev_1'}, dimensions={0} | all-to-all | bytes 2097152 | tf_op jit(solution)/shard_map/all_to_all | solution.py:17
  90.7 4.9 %collective-permute-start.1 = (f32[128,256]{1,0:T(8,128)S(1)}, f32[128,256]{1,0:T(8,128)S(1)}, u32[]{:S(2)}, u32[]{:S(2)}) collective-permute-start(f32[128,256]{1,0:T(8,128)S(1)} %get-tuple-element.9), channel_id=1, source_target_pairs={{0,1},{1,0},{2,3},{3,2},{4,5},{5,4},{6,7},{7,6},{8,9},{9,8},{10,11... | collective-permute-start | bytes 393224 | tf_op jit(solution)/shard_map/ppermute | solution.py:21
  95.6 1.0 collective-permute-done.1.other
  96.6 1.1 sum.1
  97.7 4.3 %all-to-all-start.4 = ((bf16[16,128,256]{2,1,0:T(8,128)(2,1)}), bf16[16,128,256]{2,1,0:T(8,128)(2,1)}, u32[]{:S(2)}, u32[]{:S(2)}) async-start(bf16[16,128,256]{2,1,0:T(8,128)(2,1)} %get-tuple-element.11), calls=%async_computation.4 | async-start | bytes 2097152 | tf_op jit(solution)/shard_map/all_to_all | solution.py:17
  102.0 2.3 %collective-permute-start.2 = (s32[1,256]{1,0:T(1,128)S(1)}, s32[1,256]{1,0:T(1,128)S(1)}, u32[]{:S(2)}, u32[]{:S(2)}) collective-permute-start(s32[1,256]{1,0:T(1,128)S(1)} %copy-done.9), channel_id=1, source_target_pairs={{0,1},{1,0},{2,3},{3,2},{4,5},{5,4},{6,7},{7,6},{8,9},{9,8},{10,11... | collective-permute-start | bytes 3080 | tf_op jit(solution)/shard_map/ppermute | solution.py:21
  104.3 0.8 collective-permute-done.2
  105.7 1.2 fusion.20
  108.4 10.1 %all-to-all-done.4 = bf16[16,128,256]{2,1,0:T(8,128)(2,1)} async-done(((bf16[16,128,256]{2,1,0:T(8,128)(2,1)}), bf16[16,128,256]{2,1,0:T(8,128)(2,1)}, u32[]{:S(2)}, u32[]{:S(2)}) %all-to-all-start.4) | async-done | bytes 1048608 | tf_op jit(solution)/shard_map/all_to_all | solution.py:17
  118.5 0.9 copy-done.6
  119.4 2.0 %ancestors.1 = (bf16[256,256]{1,0:T(8,128)(2,1)S(1)}, bf16[256,256]{1,0:T(8,128)(2,1)S(1)}) custom-call(s32[512,1]{1,0:T(8,128)S(1)} %get-tuple-element.17.places, bf16[2048,256]{1,0:T(8,128)(2,1)} %bitcast.9.table, bf16[512,256]{1,0:T(8,128)(2,1)S(1)} %copy-done.6), custom_call_target="tpu_custom_call" | custom-call | flops 536870912 | bytes 2097152 | tf_op jit(solution)/shard_map/ancestors/pallas_call | solution.py:40
  121.4 4.2 %collective-permute-start.3 = (bf16[256,256]{1,0:T(8,128)(2,1)S(1)}, bf16[256,256]{1,0:T(8,128)(2,1)S(1)}, u32[]{:S(2)}, u32[]{:S(2)}) collective-permute-start(bf16[256,256]{1,0:T(8,128)(2,1)S(1)} %get-tuple-element.13), channel_id=1, source_target_pairs={{0,1},{1,0},{2,3},{3,2},{4,5},{5,4},{6,7},{7,6},{8,9},{9,8},{10,11... | collective-permute-start | bytes 393224 | tf_op jit(solution)/shard_map/ppermute | solution.py:21
  126.6 1.0 copy-done.1
  127.6 1.0 copy-done.2
  128.7 1.9 %leaf.1 = bf16[1024,256]{1,0:T(8,128)(2,1)} custom-call(s32[1]{0:T(128)S(6)} %copy.49.cols, bf16[256,256]{1,0:T(8,128)(2,1)S(1)} %get-tuple-element.12.own, bf16[256,256]{1,0:T(8,128)(2,1)S(1)} %collective-permute-done.3.other, bf16[1024,256]{1,0:T(8,128)(2,1)S(1)} %copy-done.1, bf16[1024,256]{1,0:T(8,128)(2,1)S(1)} %copy-done.2, bf16[1024,1024]{1,0:T(8,128)(2,1)S(1)} %copy-done), custom_call_target="tpu_custom_call" | custom-call | flops 671088640 | bytes 4194304 | tf_op jit(solution)/shard_map/leaf/pallas_call | solution.py:40
  (30 shorter events, 5.5 us)
Async XLA Ops:
  0.6 35.7 %copy-start.7 = (bf16[128,4096]{1,0:T(8,128)(2,1)S(1)}, bf16[128,4096]{1,0:T(8,128)(2,1)}, u32[]{:S(2)}) copy-start(bf16[128,4096]{1,0:T(8,128)(2,1)} %param.14) | copy-start | bytes 3145732
  29.6 21.4 %all-to-all-start.2 = ((bf16[16,128,256]{2,1,0:T(8,128)(2,1)}), bf16[16,128,256]{2,1,0:T(8,128)(2,1)S(1)}, u32[]{:S(2)}, u32[]{:S(2)}) async-start(bf16[16,128,256]{2,1,0:T(8,128)(2,1)} %broadcast_in_dim.20), calls=%async_computation.2 | async-start | bytes 2097152 | tf_op jit(solution)/shard_map/all_to_all | solution.py:17
  36.4 19.5 %copy-start.8 = (s32[1,512]{1,0:T(1,128)S(1)}, s32[1,512]{1,0:T(1,128)}, u32[]{:S(2)}) copy-start(s32[1,512]{1,0:T(1,128)} %param.13) | copy-start | bytes 6148
  51.0 11.9 %copy-start.3 = (bf16[128,512]{1,0:T(8,128)(2,1)S(1)}, bf16[128,512]{1,0:T(8,128)(2,1)}, u32[]{:S(2)}) copy-start(bf16[128,512]{1,0:T(8,128)(2,1)} %update.2) | copy-start | bytes 393220
  51.0 11.9 %copy-start.4 = (bf16[128,256]{1,0:T(8,128)(2,1)S(1)}, bf16[128,256]{1,0:T(8,128)(2,1)}, u32[]{:S(2)}) copy-start(bf16[128,256]{1,0:T(8,128)(2,1)} %rhs.2) | copy-start | bytes 196612
  51.0 19.5 %all-to-all-start = ((bf16[16,128,256]{2,1,0:T(8,128)(2,1)}), bf16[16,128,256]{2,1,0:T(8,128)(2,1)S(1)}, u32[]{:S(2)}, u32[]{:S(2)}) async-start(bf16[16,128,256]{2,1,0:T(8,128)(2,1)} %bitcast.15), calls=%async_computation | async-start | bytes 2097152 | tf_op jit(solution)/shard_map/all_to_all | solution.py:17
  57.5 5.4 %collective-permute-start = (bf16[512,256]{1,0:T(8,128)(2,1)S(1)}, bf16[512,256]{1,0:T(8,128)(2,1)S(1)}, u32[]{:S(2)}, u32[]{:S(2)}) collective-permute-start(bf16[512,256]{1,0:T(8,128)(2,1)S(1)} %pick_sep.1.half), channel_id=1, source_target_pairs={{0,1},{1,0},{2,3},{3,2},{4,5},{5,4},{6,7},{7,6},{8,9},{9,8},{10,11... | collective-permute-start | bytes 786440 | tf_op jit(solution)/shard_map/ppermute | solution.py:21
  90.2 11.8 %copy-start.9 = (s32[1,256]{1,0:T(1,128)S(1)}, s32[1,256]{1,0:T(1,128)}, u32[]{:S(2)}) copy-start(s32[1,256]{1,0:T(1,128)} %param.17) | copy-start | bytes 3076
  90.7 5.9 %collective-permute-start.1 = (f32[128,256]{1,0:T(8,128)S(1)}, f32[128,256]{1,0:T(8,128)S(1)}, u32[]{:S(2)}, u32[]{:S(2)}) collective-permute-start(f32[128,256]{1,0:T(8,128)S(1)} %get-tuple-element.9), channel_id=1, source_target_pairs={{0,1},{1,0},{2,3},{3,2},{4,5},{5,4},{6,7},{7,6},{8,9},{9,8},{10,11... | collective-permute-start | bytes 393224 | tf_op jit(solution)/shard_map/ppermute | solution.py:21
  97.7 20.8 %all-to-all-start.4 = ((bf16[16,128,256]{2,1,0:T(8,128)(2,1)}), bf16[16,128,256]{2,1,0:T(8,128)(2,1)}, u32[]{:S(2)}, u32[]{:S(2)}) async-start(bf16[16,128,256]{2,1,0:T(8,128)(2,1)} %get-tuple-element.11), calls=%async_computation.4 | async-start | bytes 2097152 | tf_op jit(solution)/shard_map/all_to_all | solution.py:17
  102.0 3.1 %collective-permute-start.2 = (s32[1,256]{1,0:T(1,128)S(1)}, s32[1,256]{1,0:T(1,128)S(1)}, u32[]{:S(2)}, u32[]{:S(2)}) collective-permute-start(s32[1,256]{1,0:T(1,128)S(1)} %copy-done.9), channel_id=1, source_target_pairs={{0,1},{1,0},{2,3},{3,2},{4,5},{5,4},{6,7},{7,6},{8,9},{9,8},{10,11... | collective-permute-start | bytes 3080 | tf_op jit(solution)/shard_map/ppermute | solution.py:21
  106.9 19.7 %copy-start = (bf16[1024,1024]{1,0:T(8,128)(2,1)S(1)}, bf16[1024,1024]{1,0:T(8,128)(2,1)}, u32[]{:S(2)}) copy-start(bf16[1024,1024]{1,0:T(8,128)(2,1)} %inverse.1) | copy-start | bytes 6291460
  107.7 0.7 copy-start.5
  118.5 1.0 copy-start.6
  121.4 5.1 %collective-permute-start.3 = (bf16[256,256]{1,0:T(8,128)(2,1)S(1)}, bf16[256,256]{1,0:T(8,128)(2,1)S(1)}, u32[]{:S(2)}, u32[]{:S(2)}) collective-permute-start(bf16[256,256]{1,0:T(8,128)(2,1)S(1)} %get-tuple-element.13), channel_id=1, source_target_pairs={{0,1},{1,0},{2,3},{3,2},{4,5},{5,4},{6,7},{7,6},{8,9},{9,8},{10,11... | collective-permute-start | bytes 393224 | tf_op jit(solution)/shard_map/ppermute | solution.py:21
  126.6 1.0 copy-start.1
  127.6 1.0 copy-start.2

commit v2 on v1

v2 whole, which is shorter than its diff:
```python
import functools

import jax
import jax.numpy as jnp
from jax import lax
from jax.experimental import pallas as pl
from jax.experimental.pallas import tpu as pltpu
from jax.sharding import Mesh
from jax.sharding import PartitionSpec as P

ALL = ("grp", "dev_0", "dev_1", "dev_2")
XY = ("dev_0", "dev_1")
CORE = "dev_2"
BF16, F32, I32 = jnp.bfloat16, jnp.float32, jnp.int32
MIB = 1 << 20


def to_all(blocks, axes):
    return lax.all_to_all(blocks, axes, 0, 0, tiled=True)


def swapped(value):
    return lax.ppermute(value, CORE, [(0, 1), (1, 0)])


def dot(a, b, dims=((1,), (0,))):
    return lax.dot_general(a, b, (dims, ((), ())), preferred_element_type=F32)


def column(row):
    size = 128
    eye = lax.broadcasted_iota(I32, (size, size), 0) == lax.broadcasted_iota(I32, (size, size), 1)
    parts = [
        jnp.sum(jnp.where(eye, row[:, i : i + size], F32(0.0)), axis=1, keepdims=True)
        for i in range(0, row.shape[1], size)
    ]
    return jnp.concatenate(parts, axis=0)


def chosen(places, lines):
    if places.shape[0] == 1:
        places = column(places.astype(F32)).astype(I32)
    at = lax.broadcasted_iota(I32, (places.shape[0], lines), 1)
    return jnp.where(at == places, F32(1.0), F32(0.0)).astype(BF16)


def kernel_call(body, outs, flops, n_bytes, in_smem=(), limit=16, in_hbm=(), scratch=()):
    def call(*args):
        specs = [
            pl.BlockSpec(
                memory_space=pltpu.SMEM if i in in_smem else pltpu.HBM if i in in_hbm else pltpu.VMEM
            )
            for i in range(len(args))
        ]
        return pl.pallas_call(
            body,
            out_shape=outs,
            in_specs=specs,
            out_specs=jax.tree.map(lambda _: pl.BlockSpec(memory_space=pltpu.VMEM), outs),
            scratch_shapes=scratch,
            cost_estimate=pl.CostEstimate(flops=flops, bytes_accessed=n_bytes, transcendentals=0),
            compiler_params=pltpu.CompilerParams(vmem_limit_bytes=int(limit * MIB)),
        )(*args)

    return call


def log2(size):
    assert size & (size - 1) == 0
    return size.bit_length() - 1


def root_places(rows, own, cores, devices, groups):
    line = rows & (own - 1)
    device = (rows >> log2(own)) & (devices - 1)
    group = rows >> log2(own * devices)
    chip, core = device >> log2(cores), device & (cores - 1)
    return (((chip << log2(groups)) + group << log2(cores)) + core << log2(own)) + line


def side(first, value):
    half = value.shape[1] // 2
    return jnp.where(first, value[:, :half], value[:, half:])


def joined(first, mine, theirs):
    return jnp.concatenate(
        [jnp.where(first, mine, theirs), jnp.where(first, theirs, mine)], axis=1
    )


def pack_body(core, rhs, update, out):
    half = rhs.shape[1] // 2
    out[:, :half] = side(core[0] != 0, rhs[...])
    out[:, half:] = update[...]


def spread_body(sizes, core, rows, rhs, update, arrived, rhs_out, spread_out):
    half = rhs.shape[1] // 2
    rhs_out[...] = jnp.concatenate([side(core[0] == 0, rhs[...]), arrived[:, :half]], axis=0)
    both = jnp.concatenate([update[...], arrived[:, half:]], axis=0)
    at = chosen(root_places(rows[...], *sizes), spread_out.shape[1])
    spread_out[...] = dot(both, at).astype(BF16)


def terms_body(rhs, spread, table, own_inverse_at, other_inverse_at, out, own_inverse, other_inverse, sems):
    copies = (
        pltpu.make_async_copy(own_inverse_at, own_inverse, sems.at[0]),
        pltpu.make_async_copy(other_inverse_at, other_inverse, sems.at[1]),
    )
    for copy in copies:
        copy.start()
    residual = rhs[...].astype(F32) - dot(spread[...], table[...])
    residual = residual.astype(BF16).astype(F32).T.astype(BF16)
    chips, _, wide = out.shape
    for copy in copies:
        copy.wait()
    for i in range(chips):
        at = slice(i * wide, (i + 1) * wide)
        both = jnp.concatenate([own_inverse[:, at], other_inverse[:, at]], axis=0)
        out[i] = dot(residual, both).astype(BF16)


def sum_body(terms, out, copies):
    total = terms[0].astype(F32)
    for i in range(1, terms.shape[0]):
        total = total + terms[i].astype(F32)
    value = total.T.astype(BF16)
    out[...] = value
    for i in range(copies.shape[0]):
        copies[i] = value


def leaf_root_body(sizes, sep, own_rows, other_rows, table, picked_out, at_out):
    rows = jnp.concatenate([own_rows[...], other_rows[...]], axis=1)
    at = jnp.where(rows >= sep, root_places(rows - sep, *sizes), -1)
    picked_out[...] = dot(chosen(at, table.shape[0]), table[...]).astype(BF16)
    at_out[...] = column(jnp.where(rows < sep, rows, -1).astype(F32)).astype(I32)


def sep_out_body(core, value, arrived, out):
    rows = out.shape[0]
    both = value[...]
    out[...] = joined(
        core[0] == 0, jnp.where(core[0] == 0, both[:rows], both[rows:]), arrived[...]
    )


def ancestors_body(at, table, from_root, own, other):
    rows = dot(chosen(at[...], table.shape[0]), table[...])
    rows = (rows + from_root[...].astype(F32)).astype(BF16)
    half = rows.shape[0] // 2
    own[...] = rows[:half]
    other[...] = rows[half:]


def leaf_body(core, cols, own, other, rhs_at, update_at, inverse_at, out, rhs, update, inverse, sems):
    fetches = [
        pltpu.make_async_copy(source, target, sems.at[i])
        for i, (source, target) in enumerate(
            ((update_at, update), (rhs_at, rhs), (inverse_at, inverse))
        )
    ]
    for fetch in fetches:
        fetch.start()
    rows = joined(core[0] == 0, own[...], other[...])
    live = lax.broadcasted_iota(I32, out.shape, 0) < cols[0]
    fetches[0].wait()
    value = dot(update[...], rows)
    fetches[1].wait()
    residual = jnp.where(live, rhs[...].astype(F32) - value, F32(0.0)).astype(BF16)
    fetches[2].wait()
    solved = dot(inverse[...], residual)
    out[...] = jnp.where(live, solved, F32(0.0)).astype(BF16)


def on_device(
    root_solution,
    sep_rhs,
    sep_update,
    sep_rows,
    sep_inv_cols,
    leaf_rhs,
    leaf_update,
    leaf_rows,
    leaf_cols,
    leaf_inv,
):
    groups = lax.axis_size("grp")
    chips = lax.axis_size(XY)
    cores = lax.axis_size(CORE)
    devices = chips * cores
    core = lax.axis_index(CORE).astype(I32)[None]
    own_root, nrhs = root_solution.shape
    own_sep, sep = sep_inv_cols.shape
    root = own_root * groups * devices
    wide = nrhs // cores
    n_sep, n_leaf = sep_rows.shape[1], leaf_rows.shape[1]
    n_both = cores * own_sep
    sizes = (own_root, cores, devices, groups)

    def array(*shape, dtype=BF16):
        return jax.ShapeDtypeStruct(shape, dtype)

    blocks = root_solution.reshape(own_root, cores, wide).swapaxes(0, 1)
    blocks = jnp.broadcast_to(blocks, (groups, cores, own_root, wide))
    lines = to_all(blocks.reshape(groups * cores, own_root, wide), ("grp", CORE))
    lines = lines.reshape(groups * cores * own_root, wide)
    blocks = jnp.broadcast_to(lines, (chips, *lines.shape))
    root_all = to_all(blocks, XY).reshape(root, wide)

    other_inverse = swapped(sep_inv_cols)
    sent = kernel_call(
        pack_body, array(own_sep, wide + n_sep), own_sep, MIB, (0,), 4
    )(core, sep_rhs, sep_update)
    arrived = swapped(sent)
    other_rows = swapped(leaf_rows)

    rhs, spread = kernel_call(
        functools.partial(spread_body, sizes),
        (array(n_both, wide), array(n_both, root)),
        2 * n_both * n_sep * root,
        4 * MIB,
        (0,),
    )(core, sep_rows, sep_rhs, sep_update, arrived)

    terms = kernel_call(
        terms_body,
        array(chips, wide, sep // chips),
        2 * n_both * wide * (root + sep),
        6 * MIB,
        limit=16,
        in_hbm=(3, 4),
        scratch=(
            pltpu.VMEM(sep_inv_cols.shape, BF16),
            pltpu.VMEM(sep_inv_cols.shape, BF16),
            pltpu.SemaphoreType.DMA((2,)),
        ),
    )(rhs, spread, root_all, sep_inv_cols, other_inverse)
    terms = to_all(terms, XY)
    value, copies = kernel_call(
        sum_body, (array(n_both, wide), array(chips, n_both, wide)), terms.size, 2 * MIB
    )(terms)
    sep_all = to_all(copies, XY).reshape(sep, wide)

    theirs = lax.dynamic_slice_in_dim(value, (1 - core[0]) * own_sep, own_sep, 0)
    theirs = swapped(theirs)
    sep_out = kernel_call(
        sep_out_body, array(own_sep, nrhs), own_sep, MIB, (0,), 4
    )(core, value, theirs)

    leaf_root, at_leaf = kernel_call(
        functools.partial(leaf_root_body, sizes, sep),
        (array(cores * n_leaf, wide), array(cores * n_leaf, 1, dtype=I32)),
        2 * cores * n_leaf * wide * root,
        6 * MIB,
    )(leaf_rows, other_rows, root_all)
    own_rows, sent_rows = kernel_call(
        ancestors_body,
        (array(n_leaf, wide), array(n_leaf, wide)),
        2 * cores * n_leaf * wide * sep,
        6 * MIB,
    )(at_leaf, sep_all, leaf_root)
    arrived_rows = swapped(sent_rows)
    leaf_out = kernel_call(
        leaf_body,
        array(*leaf_rhs.shape),
        2 * nrhs * (leaf_inv.size + leaf_update.size),
        4 * MIB,
        (0, 1),
        limit=63.2,
        in_hbm=(4, 5, 6),
        scratch=(
            pltpu.VMEM(leaf_rhs.shape, BF16),
            pltpu.VMEM(leaf_update.shape, BF16),
            pltpu.VMEM(leaf_inv.shape, BF16),
            pltpu.SemaphoreType.DMA((3,)),
        ),
    )(core, leaf_cols, own_rows, arrived_rows, leaf_rhs, leaf_update, leaf_inv)
    return (sep_out, leaf_out)


def solution(mesh):
    finer = Mesh(mesh.devices.reshape(mesh.shape["grp"], 4, 4, 2), ALL)
    split = P(ALL, None)
    in_specs = (split, split, split, P("grp", None), split, split, split, split, P(ALL), split)
    return jax.shard_map(
        on_device, mesh=finer, in_specs=in_specs, out_specs=(split, split), check_vma=False
    )
```

time: 131 us -> 113 us (0.86)
  blocking collectives: 46.8 us -> 18.8 us
  starting transfers between devices: 31.5 us -> 45.9 us
  Pallas kernels: 7.2 us -> 13.2 us
  waiting for transfers between devices: 34.2 us -> 28.8 us
  local copies, waits for them, and re-layouts: 7.38 us -> 4.42 us
  other arithmetic: 1.94 us -> 0 us
    all_to_all x2 -> x1, blocking collectives: 46.8 us -> 18.8 us  [to_all(): return lax.all_to_all(blocks, axes, 0, 0, tiled=True)]
    all_to_all x3, starting transfers between devices: 16 us -> 27.1 us  [to_all(): return lax.all_to_all(blocks, axes, 0, 0, tiled=True)]
    pallas_call x7 -> x8, Pallas kernels: 7.2 us -> 13.2 us  [call(): pl.pallas_call(body, out_shape=outs, in_specs=specs, out_specs=jax.tree.m...]
    all_to_all x3, waiting for transfers between devices: 31 us -> 26.5 us  [to_all(): return lax.all_to_all(blocks, axes, 0, 0, tiled=True)]
    ppermute x4 -> x5, starting transfers between devices: 15.6 us -> 18.7 us  [swapped(): return lax.ppermute(value, CORE, [(0, 1), (1, 0)])]
    select_n x2 -> x0, other arithmetic: 1.92 us -> none  [the longest x1 1.23 us: on_device(): jnp.where(both_rows >= sep, root_places(both_rows - sep), -1)[:, None]]
    unnamed x20 -> x14, local copies, waits for them, and re-layouts: 3.76 us -> 1.86 us
    ppermute x4 -> x5, waiting for transfers between devices: 3.22 us -> 2.33 us  [swapped(): return lax.ppermute(value, CORE, [(0, 1), (1, 0)])]
  transfers between devices with their start and end apart: 7 -> 8, of which waited for: 7 -> 6; matrix products, arithmetic and copies ran while one was open for 3% -> 1% of each run, Pallas kernels for 1% -> 3%
where the time goes in v2:
time: 113 us
  starting transfers between devices  45.9 us (41%)
  waiting for transfers between devices  28.8 us (25%)
  blocking collectives  18.8 us (17%)
  Pallas kernels  13.2 us (12%)
  local copies, waits for them, and re-layouts  4.42 us (4%)
  between operations  1.47 us (1%)
    all_to_all x3, starting transfers between devices, to_all(): return lax.all_to_all(blocks, axes, 0, 0, tiled=True)  27.1 us
    all_to_all x3, waiting for transfers between devices, to_all(): return lax.all_to_all(blocks, axes, 0, 0, tiled=True)  26.5 us
    all_to_all x1, blocking collectives, to_all(): return lax.all_to_all(blocks, axes, 0, 0, tiled=True)  18.8 us
    ppermute x5, starting transfers between devices, swapped(): return lax.ppermute(value, CORE, [(0, 1), (1, 0)])  18.7 us
    pallas_call x8, Pallas kernels, call(): pl.pallas_call(body, out_shape=outs, in_specs=specs, out_specs=jax.tree.m...  13.2 us
    ppermute x5, waiting for transfers between devices, swapped(): return lax.ppermute(value, CORE, [(0, 1), (1, 0)])  2.33 us
  transfers between devices with their start and end apart: 8, of which 6 were waited for; matrix products, arithmetic and copies ran while one was open for 1% of the time, Pallas kernels for 3%

profile of v2, /device:TPU:1, one launch (start us, length us, event | category | flops | bytes accessed | tf_op | source)
XLA Modules:
  0.0 112.6 jit_solution(11178047866508321479)
XLA Ops:
  0.7 1.4 %broadcast_in_dim.10 = bf16[16,2,8,128]{3,2,1,0:T(8,128)(2,1)} broadcast(bf16[2,8,128]{2,1,0:T(8,128)(2,1)} %bitcast.12), dimensions={1,2,3} | broadcast | bytes 69632 | tf_op jit(solution)/shard_map/broadcast_in_dim | solution.py:206
  2.0 16.7 %all-to-all-start = ((bf16[32,8,128]{2,1,0:T(8,128)(2,1)}), bf16[32,8,128]{2,1,0:T(8,128)(2,1)S(1)}, u32[]{:S(2)}, u32[]{:S(2)}) async-start(bf16[32,8,128]{2,1,0:T(8,128)(2,1)} %bitcast.3), calls=%async_computation | async-start | bytes 131072 | tf_op jit(solution)/shard_map/all_to_all | solution.py:19
  18.8 2.1 %collective-permute-start.1 = (bf16[128,4096]{1,0:T(8,128)(2,1)}, bf16[128,4096]{1,0:T(8,128)(2,1)}, u32[]{:S(2)}, u32[]{:S(2)}) collective-permute-start(bf16[128,4096]{1,0:T(8,128)(2,1)} %own_inverse_at.1), channel_id=1, source_target_pairs={{0,1},{1,0},{2,3},{3,2},{4,5},{5,4},{6,7},{7,6},{8,9},{9,8},{10,11... | collective-permute-start | bytes 3145736 | tf_op jit(solution)/shard_map/ppermute | solution.py:23
  20.9 10.9 %all-to-all-done = bf16[32,8,128]{2,1,0:T(8,128)(2,1)S(1)} async-done(((bf16[32,8,128]{2,1,0:T(8,128)(2,1)}), bf16[32,8,128]{2,1,0:T(8,128)(2,1)S(1)}, u32[]{:S(2)}, u32[]{:S(2)}) %all-to-all-start) | async-done | bytes 65568 | tf_op jit(solution)/shard_map/all_to_all | solution.py:19
  31.8 1.2 %broadcast_in_dim.11 = bf16[16,256,128]{2,1,0:T(8,128)(2,1)} broadcast(bf16[256,128]{1,0:T(8,128)(2,1)S(1)} %bitcast.11), dimensions={1,2} | broadcast | bytes 1114112 | tf_op jit(solution)/shard_map/broadcast_in_dim | solution.py:209
  33.0 6.8 %all-to-all-start.1 = ((bf16[16,256,128]{2,1,0:T(8,128)(2,1)}), bf16[16,256,128]{2,1,0:T(8,128)(2,1)S(1)}, u32[]{:S(2)}, u32[]{:S(2)}) async-start(bf16[16,256,128]{2,1,0:T(8,128)(2,1)} %broadcast_in_dim.11), calls=%async_computation.1 | async-start | bytes 2097152 | tf_op jit(solution)/shard_map/all_to_all | solution.py:19
  39.8 3.8 %collective-permute-start = (bf16[128,640]{1,0:T(8,128)(2,1)S(1)}, bf16[128,640]{1,0:T(8,128)(2,1)S(1)}, u32[]{:S(2)}, u32[]{:S(2)}) collective-permute-start(bf16[128,640]{1,0:T(8,128)(2,1)S(1)} %shard_map.113), channel_id=1, source_target_pairs={{0,1},{1,0},{2,3},{3,2},{4,5},{5,4},{6,7},{7,6},{8,9},{9,8},{10,11... | collective-permute-start | bytes 491528 | tf_op jit(solution)/shard_map/ppermute | solution.py:23
  43.6 1.0 collective-permute-done.arrived
  44.6 1.5 %shard_map.114 = (bf16[256,128]{1,0:T(8,128)(2,1)S(1)}, bf16[256,4096]{1,0:T(8,128)(2,1)S(1)}) custom-call(s32[1]{0:T(128)} %bitcast.core, s32[1,512]{1,0:T(1,128)S(1)} %copy-done.4, bf16[128,256]{1,0:T(8,128)(2,1)S(1)} %copy-done.3, bf16[128,512]{1,0:T(8,128)(2,1)S(1)} %copy-done.1, bf16[128,640]{1,0:T(8,128)(2,1)S(1)} %collective-permute-done.arrived), custom_call_target="tpu_custom_call" | custom-call | flops 1073741824 | bytes 4194304 | tf_op jit(solution)/shard_map/pallas_call | solution.py:55
  46.1 8.7 %all-to-all-done.1 = bf16[16,256,128]{2,1,0:T(8,128)(2,1)S(1)} async-done(((bf16[16,256,128]{2,1,0:T(8,128)(2,1)}), bf16[16,256,128]{2,1,0:T(8,128)(2,1)S(1)}, u32[]{:S(2)}, u32[]{:S(2)}) %all-to-all-start.1) | async-done | bytes 1048608 | tf_op jit(solution)/shard_map/all_to_all | solution.py:19
  54.9 1.2 %copy-done = bf16[128,4096]{1,0:T(8,128)(2,1)S(1)} copy-done((bf16[128,4096]{1,0:T(8,128)(2,1)S(1)}, bf16[128,4096]{1,0:T(8,128)(2,1)}, u32[]{:S(2)}) %copy-start) | copy-done | bytes 1048600
  56.1 2.4 %shard_map.115 = bf16[16,128,256]{2,1,0:T(8,128)(2,1)S(1)} custom-call(bf16[256,128]{1,0:T(8,128)(2,1)S(1)} %get-tuple-element.10.rhs, bf16[256,4096]{1,0:T(8,128)(2,1)S(1)} %get-tuple-element.11.spread, bf16[4096,128]{1,0:T(8,128)(2,1)S(1)} %bitcast.8, bf16[128,4096]{1,0:T(8,128)(2,1)S(1)} %copy-done, bf16[128,4096]{1,0:T(8,128)(2,1)} %collective-permute-done.1.other_inverse_at), custom_call_target="tpu_custom_call" | custom-call | flops 536870912 | bytes 6291456 | tf_op jit(solution)/shard_map/pallas_call | solution.py:55
  58.5 18.8 %all_to_all.20.terms = bf16[16,128,256]{2,1,0:T(8,128)(2,1)S(1)} all-to-all(bf16[16,128,256]{2,1,0:T(8,128)(2,1)S(1)} %shard_map.115), channel_id=1, replica_groups=mesh['grp'=16,'dev_0'=4,'dev_1'=4,'dev_2'=2] {'dev_0','dev_1'}, dimensions={0} | all-to-all | bytes 2097152 | tf_op jit(solution)/shard_map/all_to_all | solution.py:19
  77.4 1.3 %shard_map.116 = (bf16[256,128]{1,0:T(8,128)(2,1)S(1)}, bf16[16,256,128]{2,1,0:T(8,128)(2,1)}) custom-call(bf16[16,128,256]{2,1,0:T(8,128)(2,1)S(1)} %all_to_all.20.terms), custom_call_target="tpu_custom_call" | custom-call | flops 524288 | bytes 2097152 | tf_op jit(solution)/shard_map/pallas_call | solution.py:55
  78.7 3.7 %all-to-all-start.3 = ((bf16[16,256,128]{2,1,0:T(8,128)(2,1)}), bf16[16,256,128]{2,1,0:T(8,128)(2,1)S(1)}, u32[]{:S(2)}, u32[]{:S(2)}) async-start(bf16[16,256,128]{2,1,0:T(8,128)(2,1)} %get-tuple-element.14), calls=%async_computation.3 | async-start | bytes 2097152 | tf_op jit(solution)/shard_map/all_to_all | solution.py:19
  82.3 5.0 %collective-permute-start.3 = (s32[1,256]{1,0:T(1,128)S(1)}, s32[1,256]{1,0:T(1,128)S(1)}, u32[]{:S(2)}, u32[]{:S(2)}) collective-permute-start(s32[1,256]{1,0:T(1,128)S(1)} %copy-done.5), channel_id=1, source_target_pairs={{0,1},{1,0},{2,3},{3,2},{4,5},{5,4},{6,7},{7,6},{8,9},{9,8},{10,11... | collective-permute-start | bytes 3080 | tf_op jit(solution)/shard_map/ppermute | solution.py:23
  87.4 0.8 collective-permute-done.3.other_rows
  88.2 1.5 %shard_map.118 = (bf16[512,128]{1,0:T(8,128)(2,1)S(1)}, s32[512,1]{1,0:T(8,128)S(1)}) custom-call(s32[1,256]{1,0:T(1,128)S(1)} %copy-done.5, s32[1,256]{1,0:T(1,128)S(1)} %collective-permute-done.3.other_rows, bf16[4096,128]{1,0:T(8,128)(2,1)S(1)} %bitcast.9), custom_call_target="tpu_custom_call" | custom-call | flops 536870912 | bytes 6291456 | tf_op jit(solution)/shard_map/pallas_call | solution.py:55
  89.7 6.9 %all-to-all-done.3 = bf16[16,256,128]{2,1,0:T(8,128)(2,1)S(1)} async-done(((bf16[16,256,128]{2,1,0:T(8,128)(2,1)}), bf16[16,256,128]{2,1,0:T(8,128)(2,1)S(1)}, u32[]{:S(2)}, u32[]{:S(2)}) %all-to-all-start.3) | async-done | bytes 1048608 | tf_op jit(solution)/shard_map/all_to_all | solution.py:19
  96.6 1.3 %shard_map.119 = (bf16[256,128]{1,0:T(8,128)(2,1)S(1)}, bf16[256,128]{1,0:T(8,128)(2,1)S(1)}) custom-call(s32[512,1]{1,0:T(8,128)S(1)} %get-tuple-element.13.at, bf16[4096,128]{1,0:T(8,128)(2,1)S(1)} %bitcast.10, bf16[512,128]{1,0:T(8,128)(2,1)S(1)} %get-tuple-element.15.from_root), custom_call_target="tpu_custom_call" | custom-call | flops 536870912 | bytes 6291456 | tf_op jit(solution)/shard_map/pallas_call | solution.py:55
  97.9 5.9 %collective-permute-start.4 = (bf16[256,128]{1,0:T(8,128)(2,1)S(1)}, bf16[256,128]{1,0:T(8,128)(2,1)S(1)}, u32[]{:S(2)}, u32[]{:S(2)}) collective-permute-start(bf16[256,128]{1,0:T(8,128)(2,1)S(1)} %get-tuple-element.17), channel_id=1, source_target_pairs={{0,1},{1,0},{2,3},{3,2},{4,5},{5,4},{6,7},{7,6},{8,9},{9,8},{10,11... | collective-permute-start | bytes 196616 | tf_op jit(solution)/shard_map/ppermute | solution.py:23
  103.7 1.9 %collective-permute-start.2 = (bf16[128,128]{1,0:T(8,128)(2,1)S(1)}, bf16[128,128]{1,0:T(8,128)(2,1)S(1)}, u32[]{:S(2)}, u32[]{:S(2)}) collective-permute-start(bf16[128,128]{1,0:T(8,128)(2,1)S(1)} %constant_dynamic-slice_fusion), channel_id=1, source_target_pairs={{0,1},{1,0},{2,3},{3,2},{4,5},{5,4},{6,7},{7,6},{8,9},{9,8},{10,11... | collective-permute-start | bytes 98312 | tf_op jit(solution)/shard_map/ppermute | solution.py:23
  106.8 0.6 shard_map.117
  108.1 4.5 %shard_map.120 = bf16[1024,256]{1,0:T(8,128)(2,1)} custom-call(s32[1]{0:T(128)} %bitcast.core, s32[1]{0:T(128)S(6)} %copy.12.cols, bf16[256,128]{1,0:T(8,128)(2,1)} %copy-done.2, bf16[256,128]{1,0:T(8,128)(2,1)} %copy-done.6, bf16[1024,256]{1,0:T(8,128)(2,1)} %rhs_at.1, bf16[1024,256]{1,0:T(8,128)(2,1)} %update_at.1, bf16[1024,1024]{1,0:T(8,128)(2,1)} %inverse_at.1), custom_call_target="tpu_custom_call" | custom-call | flops 671088640 | bytes 4194304 | tf_op jit(solution)/shard_map/pallas_call | solution.py:55
  (18 shorter events, 1.2 us)
Async XLA Ops:
  0.6 39.1 %copy-start.3 = (bf16[128,256]{1,0:T(8,128)(2,1)S(1)}, bf16[128,256]{1,0:T(8,128)(2,1)}, u32[]{:S(2)}) copy-start(bf16[128,256]{1,0:T(8,128)(2,1)} %rhs.3) | copy-start | bytes 196612
  0.6 39.1 %copy-start.1 = (bf16[128,512]{1,0:T(8,128)(2,1)S(1)}, bf16[128,512]{1,0:T(8,128)(2,1)}, u32[]{:S(2)}) copy-start(bf16[128,512]{1,0:T(8,128)(2,1)} %update.3) | copy-start | bytes 393220
  0.7 43.9 %copy-start.4 = (s32[1,512]{1,0:T(1,128)S(1)}, s32[1,512]{1,0:T(1,128)}, u32[]{:S(2)}) copy-start(s32[1,512]{1,0:T(1,128)} %rows.1) | copy-start | bytes 6148
  2.0 29.8 %all-to-all-start = ((bf16[32,8,128]{2,1,0:T(8,128)(2,1)}), bf16[32,8,128]{2,1,0:T(8,128)(2,1)S(1)}, u32[]{:S(2)}, u32[]{:S(2)}) async-start(bf16[32,8,128]{2,1,0:T(8,128)(2,1)} %bitcast.3), calls=%async_computation | async-start | bytes 131072 | tf_op jit(solution)/shard_map/all_to_all | solution.py:19
  18.8 27.3 %collective-permute-start.1 = (bf16[128,4096]{1,0:T(8,128)(2,1)}, bf16[128,4096]{1,0:T(8,128)(2,1)}, u32[]{:S(2)}, u32[]{:S(2)}) collective-permute-start(bf16[128,4096]{1,0:T(8,128)(2,1)} %own_inverse_at.1), channel_id=1, source_target_pairs={{0,1},{1,0},{2,3},{3,2},{4,5},{5,4},{6,7},{7,6},{8,9},{9,8},{10,11... | collective-permute-start | bytes 3145736 | tf_op jit(solution)/shard_map/ppermute | solution.py:23
  33.0 21.9 %all-to-all-start.1 = ((bf16[16,256,128]{2,1,0:T(8,128)(2,1)}), bf16[16,256,128]{2,1,0:T(8,128)(2,1)S(1)}, u32[]{:S(2)}, u32[]{:S(2)}) async-start(bf16[16,256,128]{2,1,0:T(8,128)(2,1)} %broadcast_in_dim.11), calls=%async_computation.1 | async-start | bytes 2097152 | tf_op jit(solution)/shard_map/all_to_all | solution.py:19
  39.8 4.8 %collective-permute-start = (bf16[128,640]{1,0:T(8,128)(2,1)S(1)}, bf16[128,640]{1,0:T(8,128)(2,1)S(1)}, u32[]{:S(2)}, u32[]{:S(2)}) collective-permute-start(bf16[128,640]{1,0:T(8,128)(2,1)S(1)} %shard_map.113), channel_id=1, source_target_pairs={{0,1},{1,0},{2,3},{3,2},{4,5},{5,4},{6,7},{7,6},{8,9},{9,8},{10,11... | collective-permute-start | bytes 491528 | tf_op jit(solution)/shard_map/ppermute | solution.py:23
  54.9 1.2 %copy-start = (bf16[128,4096]{1,0:T(8,128)(2,1)S(1)}, bf16[128,4096]{1,0:T(8,128)(2,1)}, u32[]{:S(2)}) copy-start(bf16[128,4096]{1,0:T(8,128)(2,1)} %own_inverse_at.1) | copy-start | bytes 3145732
  77.4 5.0 %copy-start.5 = (s32[1,256]{1,0:T(1,128)S(1)}, s32[1,256]{1,0:T(1,128)}, u32[]{:S(2)}) copy-start(s32[1,256]{1,0:T(1,128)} %own_rows.1) | copy-start | bytes 3076
  78.7 17.9 %all-to-all-start.3 = ((bf16[16,256,128]{2,1,0:T(8,128)(2,1)}), bf16[16,256,128]{2,1,0:T(8,128)(2,1)S(1)}, u32[]{:S(2)}, u32[]{:S(2)}) async-start(bf16[16,256,128]{2,1,0:T(8,128)(2,1)} %get-tuple-element.14), calls=%async_computation.3 | async-start | bytes 2097152 | tf_op jit(solution)/shard_map/all_to_all | solution.py:19
  82.3 5.8 %collective-permute-start.3 = (s32[1,256]{1,0:T(1,128)S(1)}, s32[1,256]{1,0:T(1,128)S(1)}, u32[]{:S(2)}, u32[]{:S(2)}) collective-permute-start(s32[1,256]{1,0:T(1,128)S(1)} %copy-done.5), channel_id=1, source_target_pairs={{0,1},{1,0},{2,3},{3,2},{4,5},{5,4},{6,7},{7,6},{8,9},{9,8},{10,11... | collective-permute-start | bytes 3080 | tf_op jit(solution)/shard_map/ppermute | solution.py:23
  97.9 9.6 %copy-start.2 = (bf16[256,128]{1,0:T(8,128)(2,1)}, bf16[256,128]{1,0:T(8,128)(2,1)S(1)}, u32[]{:S(2)}) copy-start(bf16[256,128]{1,0:T(8,128)(2,1)S(1)} %get-tuple-element.16.own) | copy-start | bytes 196612
  97.9 9.6 %collective-permute-start.4 = (bf16[256,128]{1,0:T(8,128)(2,1)S(1)}, bf16[256,128]{1,0:T(8,128)(2,1)S(1)}, u32[]{:S(2)}, u32[]{:S(2)}) collective-permute-start(bf16[256,128]{1,0:T(8,128)(2,1)S(1)} %get-tuple-element.17), channel_id=1, source_target_pairs={{0,1},{1,0},{2,3},{3,2},{4,5},{5,4},{6,7},{7,6},{8,9},{9,8},{10,11... | collective-permute-start | bytes 196616 | tf_op jit(solution)/shard_map/ppermute | solution.py:23
  103.7 3.1 %collective-permute-start.2 = (bf16[128,128]{1,0:T(8,128)(2,1)S(1)}, bf16[128,128]{1,0:T(8,128)(2,1)S(1)}, u32[]{:S(2)}, u32[]{:S(2)}) collective-permute-start(bf16[128,128]{1,0:T(8,128)(2,1)S(1)} %constant_dynamic-slice_fusion), channel_id=1, source_target_pairs={{0,1},{1,0},{2,3},{3,2},{4,5},{5,4},{6,7},{7,6},{8,9},{9,8},{10,11... | collective-permute-start | bytes 98312 | tf_op jit(solution)/shard_map/ppermute | solution.py:23
  107.5 0.6 copy-start.6

commit v3 on v2

v3 whole, which is shorter than its diff:
```python
import functools

import jax
import jax.numpy as jnp
from jax import lax
from jax.experimental import pallas as pl
from jax.experimental.pallas import tpu as pltpu
from jax.sharding import Mesh
from jax.sharding import PartitionSpec as P

ALL = ("grp", "dev_0", "dev_1", "dev_2")
XY = ("dev_0", "dev_1")
SLOTS, LIST = 64, 8
BASE = 64
CORE = "dev_2"
BF16, F32, I32 = jnp.bfloat16, jnp.float32, jnp.int32
MIB = 1 << 20


def to_all(blocks, axes):
    return lax.all_to_all(blocks, axes, 0, 0, tiled=True)


def swapped(value):
    return lax.ppermute(value, CORE, [(0, 1), (1, 0)])


def dot(a, b, dims=((1,), (0,))):
    return lax.dot_general(a, b, (dims, ((), ())), preferred_element_type=F32)


def column(row):
    size = 128
    eye = lax.broadcasted_iota(I32, (size, size), 0) == lax.broadcasted_iota(I32, (size, size), 1)
    parts = [
        jnp.sum(jnp.where(eye, row[:, i : i + size], F32(0.0)), axis=1, keepdims=True)
        for i in range(0, row.shape[1], size)
    ]
    return jnp.concatenate(parts, axis=0)


def chosen(places, lines):
    if places.shape[0] == 1:
        places = column(places.astype(F32)).astype(I32)
    at = lax.broadcasted_iota(I32, (places.shape[0], lines), 1)
    return jnp.where(at == places, F32(1.0), F32(0.0)).astype(BF16)


def kernel_call(body, outs, flops, n_bytes, in_smem=(), limit=16, in_hbm=(), scratch=()):
    def call(*args):
        specs = [
            pl.BlockSpec(
                memory_space=pltpu.SMEM if i in in_smem else pltpu.HBM if i in in_hbm else pltpu.VMEM
            )
            for i in range(len(args))
        ]
        return pl.pallas_call(
            body,
            out_shape=outs,
            in_specs=specs,
            out_specs=jax.tree.map(
                lambda out: pl.BlockSpec(
                    memory_space=pltpu.SMEM if out.ndim == 1 else pltpu.VMEM
                ),
                outs,
            ),
            scratch_shapes=scratch,
            cost_estimate=pl.CostEstimate(
                flops=flops, bytes_accessed=n_bytes, transcendentals=0
            ),
            compiler_params=pltpu.CompilerParams(vmem_limit_bytes=int(limit * MIB)),
        )(*args)

    return call


def log2(size):
    assert size & (size - 1) == 0
    return size.bit_length() - 1


def root_owner(rows, own, cores, devices, groups):
    device = (rows >> log2(own)) & (devices - 1)
    line = ((rows >> log2(own * devices)) << log2(cores)) + (device & (cores - 1))
    return device >> log2(cores), (line << log2(own)) + (rows & (own - 1))


def ancestor_owner(sizes, sep, held, rows):
    chip, line = root_owner(rows - sep, *sizes)
    here = rows < sep
    return jnp.where(here, rows >> log2(held), chip), jnp.where(here, rows & (held - 1), held + line)


def before(size):
    lines = lax.broadcasted_iota(I32, (size, size), 0)
    return one(lines < lax.broadcasted_iota(I32, (size, size), 1))


def one(mask):
    return jnp.where(mask, F32(1.0), F32(0.0)).astype(BF16)


def encoded(rows):
    digits = [rows >> log2(BASE), rows & (BASE - 1)]
    size = 128
    lines = [d[:, i : i + size] for d in digits for i in range(0, rows.shape[1], size)]
    return jnp.concatenate(lines, axis=0).astype(F32).astype(BF16)


def decoded(lines):
    value = lines.astype(F32)
    half = value.shape[0] // 2
    value = value[:half] * F32(BASE) + value[half:]
    return jnp.concatenate([value[i : i + 1] for i in range(half)], axis=1).astype(I32)


def side(first, value):
    half = value.shape[1] // 2
    return jnp.where(first, value[:, :half], value[:, half:])


def of_core(first, value):
    half = value.shape[0] // 2
    return jnp.where(first, value[:half], value[half:])


def joined(first, mine, theirs):
    return jnp.concatenate(
        [jnp.where(first, mine, theirs), jnp.where(first, theirs, mine)], axis=1
    )


def fan_body(root, out):
    half = root.shape[1] // 2
    low, high = root[:, :half], root[:, half:]
    for i in range(0, out.shape[0], 2):
        out[i] = low
        out[i + 1] = high


def pack_body(core, rhs, update, leaf_rows, out):
    rows, half = rhs.shape[0], rhs.shape[1] // 2
    out[:rows, :half] = side(core[0] != 0, rhs[...])
    out[:rows, half:] = update[...]
    listed = leaf_rows[...]
    digits = jnp.concatenate([listed >> log2(BASE), listed & (BASE - 1)], axis=1)
    spare = out.shape[0] - rows
    digits = jnp.broadcast_to(digits.astype(F32), (spare, digits.shape[1]))
    out[rows:, : digits.shape[1]] = digits.astype(BF16)
    out[rows:, digits.shape[1] :] = jnp.zeros((spare, out.shape[1] - digits.shape[1]), BF16)


def plan_body(
    sizes, me, rows, rhs, update, leaf_rows, arrived, rhs_out, spread_out, select_out, list_out, fits_out
):
    own, half = rhs.shape[0], rhs.shape[1] // 2
    core, chip = me[0], me[1]
    rhs_out[...] = jnp.concatenate([side(core == 0, rhs[...]), arrived[:own, :half]], axis=0)
    both = jnp.concatenate([update[...], arrived[:own, half:]], axis=0)

    chips = spread_out.shape[1] // SLOTS
    wanted = rows[...]
    size = wanted.shape[1]
    owner, line = root_owner(wanted, *sizes)
    owned = lax.broadcasted_iota(I32, (chips, size), 0) == owner
    rank = jnp.where(owned, dot(one(owned), before(size)), F32(0.0))
    rank = jnp.sum(rank, axis=0, keepdims=True).astype(I32)
    most = jnp.max(rank.astype(F32))
    fits = (most < F32(SLOTS)).astype(I32)
    fits_out[0] = fits
    place = jnp.where(fits == 1, owner * SLOTS + rank, lax.broadcasted_iota(I32, (1, size), 1))
    spread_out[...] = dot(both, chosen(place, spread_out.shape[1])).astype(BF16)

    mine = jnp.where(owner == chip, rank, -1)
    slot = one(lax.broadcasted_iota(I32, (SLOTS, size), 0) == mine)
    lines = select_out.shape[1]
    source = one(lax.broadcasted_iota(I32, (lines, size), 0) == line)
    select_out[...] = dot(slot, source, ((1,), (1,))).astype(BF16)

    n_leaf = leaf_rows.shape[1]
    digits = arrived[own:, : 2 * n_leaf].astype(F32)[:1]
    other = (digits[:, :n_leaf] * F32(BASE) + digits[:, n_leaf:]).astype(I32)
    list_out[...] = encoded(jnp.concatenate([leaf_rows[...], other], axis=1))


def select_body(select, lines, listed, out):
    rows = dot(select[...], lines[...]).astype(BF16)
    listed = listed[...]
    for i in range(out.shape[0]):
        out[i, :SLOTS] = rows
        out[i, SLOTS:] = listed


def all_lines_body(lines, listed, out):
    held = lines.shape[0]
    for i in range(out.shape[0]):
        out[i, :held] = lines[...]
        out[i, held:] = listed[...]


def all_rows_body(sizes, rows, arrived, out):
    chips, held, wide = arrived.shape
    held = held - LIST
    owner, line = root_owner(rows[...], *sizes)
    table = arrived[:, :held].reshape(chips * held, wide)
    picked = dot(chosen(owner * held + line, chips * held), table).astype(BF16)
    full = picked.shape[0] // SLOTS
    out[:full, :SLOTS] = picked.reshape(full, SLOTS, wide)
    out[full:, :SLOTS] = jnp.zeros((chips - full, SLOTS, wide), BF16)
    out[:, SLOTS:] = arrived[:, held:]


def terms_body(rhs, spread, arrived, own_inverse_at, other_inverse_at, out, own_inverse, other_inverse, sems):
    copies = (
        pltpu.make_async_copy(own_inverse_at, own_inverse, sems.at[0]),
        pltpu.make_async_copy(other_inverse_at, other_inverse, sems.at[1]),
    )
    for copy in copies:
        copy.start()
    chips, _, width = out.shape
    wide = rhs.shape[1]
    table = arrived[:, :SLOTS].reshape(chips * SLOTS, wide)
    residual = rhs[...].astype(F32) - dot(spread[...], table)
    residual = residual.astype(BF16).astype(F32).T.astype(BF16)
    for copy in copies:
        copy.wait()
    for i in range(chips):
        at = slice(i * width, (i + 1) * width)
        both = jnp.concatenate([own_inverse[:, at], other_inverse[:, at]], axis=0)
        out[i] = dot(residual, both).astype(BF16)


def leaf_plan_body(sizes, sep, held, me, arrived, select_out, place_out, fits_out, mine_at, line_at):
    chips = arrived.shape[0]
    chip = me[1]
    rows = jnp.concatenate([decoded(arrived[i, SLOTS:]) for i in range(chips)], axis=0)
    size = rows.shape[1]
    owner, line = ancestor_owner(sizes, sep, held, rows)
    counts = before(size)
    owned = jnp.concatenate([owner == i for i in range(chips)], axis=0)
    rank = jnp.where(owned, dot(one(owned), counts), F32(0.0))
    fits = (jnp.max(rank) < F32(SLOTS)).astype(I32)
    fits_out[0] = fits

    listed = lax.broadcasted_iota(I32, (chips, 1), 0) == chip
    own_rank = jnp.zeros((1, size), F32)
    for i in range(chips):
        part = rank[i * chips : (i + 1) * chips]
        own_rank = own_rank + jnp.sum(jnp.where(listed, part, F32(0.0)), axis=0, keepdims=True)
    own_owner = jnp.sum(jnp.where(listed, owner.astype(F32), F32(0.0)), axis=0, keepdims=True)
    place = own_owner * F32(SLOTS) + own_rank
    place = jnp.where(fits == 1, place, lax.broadcasted_iota(I32, (1, size), 1).astype(F32))
    place_out[...] = column(place).astype(I32)

    mine = owner == chip
    mine_at[...] = jnp.where(mine, dot(one(mine), counts), F32(-1.0)).astype(I32)
    line_at[...] = line

    def step(i, _):
        slot = one(lax.broadcasted_iota(I32, (SLOTS, size), 0) == mine_at[pl.ds(i, 1), :])
        lines = select_out.shape[2]
        source = one(lax.broadcasted_iota(I32, (lines, size), 0) == line_at[pl.ds(i, 1), :])
        select_out[i] = dot(slot, source, ((1,), (1,))).astype(BF16)
        return 0

    lax.fori_loop(0, chips, step, 0)


def sum_body(terms, select, lines, out, blocks):
    total = terms[0].astype(F32)
    for i in range(1, terms.shape[0]):
        total = total + terms[i].astype(F32)
    value = total.T.astype(BF16)
    out[...] = value
    table = jnp.concatenate([value, lines[...]], axis=0)
    chips, slots, size = select.shape
    rows = dot(select[...].reshape(chips * slots, size), table).astype(BF16)
    blocks[...] = rows.reshape(blocks.shape)


def all_ancestors_body(sizes, sep, held, listed, arrived, out):
    chips, lines, wide = arrived.shape
    owner, line = ancestor_owner(sizes, sep, held, decoded(listed[...]))
    place = owner * lines + line
    total = jnp.zeros((place.shape[1], wide), F32)
    for i in range(chips):
        total = total + dot(chosen(place - i * lines, lines), arrived[i])
    full = total.shape[0] // SLOTS
    out[:full] = total.astype(BF16).reshape(full, SLOTS, wide)
    out[full:] = jnp.zeros((chips - full, SLOTS, wide), BF16)


def ancestors_body(me, place, arrived, value, own, sent):
    chips, slots, wide = arrived.shape
    table = arrived[...].reshape(chips * slots, wide)
    rows = dot(chosen(place[...], chips * slots), table).astype(BF16)
    half = rows.shape[0] // 2
    own[...] = rows[:half]
    sent[:half] = rows[half:]
    sent[half:] = of_core(me[0] != 0, value[...])


def leaf_body(
    me, cols, own, arrived, value, rhs_at, update_at, inverse_at, out, sep_out, rhs, update, inverse, sems
):
    fetches = [
        pltpu.make_async_copy(source, target, sems.at[i])
        for i, (source, target) in enumerate(
            ((update_at, update), (rhs_at, rhs), (inverse_at, inverse))
        )
    ]
    for fetch in fetches:
        fetch.start()
    first, half = me[0] == 0, own.shape[0]
    rows = joined(first, own[...], arrived[:half])
    sep_out[...] = joined(first, of_core(first, value[...]), arrived[half:])
    live = lax.broadcasted_iota(I32, out.shape, 0) < cols[0]
    fetches[0].wait()
    term = dot(update[...], rows)
    fetches[1].wait()
    residual = jnp.where(live, rhs[...].astype(F32) - term, F32(0.0)).astype(BF16)
    fetches[2].wait()
    solved = dot(inverse[...], residual)
    out[...] = jnp.where(live, solved, F32(0.0)).astype(BF16)


def on_device(
    root_solution,
    sep_rhs,
    sep_update,
    sep_rows,
    sep_inv_cols,
    leaf_rhs,
    leaf_update,
    leaf_rows,
    leaf_cols,
    leaf_inv,
):
    groups = lax.axis_size("grp")
    chips = lax.axis_size(XY)
    cores = lax.axis_size(CORE)
    devices = chips * cores
    me = jnp.stack([lax.axis_index(CORE), lax.axis_index(XY)]).astype(I32)
    own_root, nrhs = root_solution.shape
    own_sep, sep = sep_inv_cols.shape
    wide = nrhs // cores
    n_sep, n_leaf = sep_rows.shape[1], leaf_rows.shape[1]
    held = cores * own_sep
    lines_here = groups * cores * own_root
    sizes = (own_root, cores, devices, groups)

    def array(*shape, dtype=BF16):
        return jax.ShapeDtypeStruct(shape, dtype)

    flag = array(1, dtype=I32)

    blocks = kernel_call(fan_body, array(groups * cores, own_root, wide), 1024, MIB, limit=4)(
        root_solution
    )
    lines = to_all(blocks, ("grp", CORE)).reshape(lines_here, wide)

    other_inverse = swapped(sep_inv_cols)
    sent = kernel_call(
        pack_body, array(own_sep + 8, wide + n_sep), own_sep, MIB, (0,), 4
    )(me, sep_rhs, sep_update, leaf_rows)
    arrived = swapped(sent)

    rhs, spread, select, listed, fits = kernel_call(
        functools.partial(plan_body, sizes),
        (
            array(held, wide),
            array(held, chips * SLOTS),
            array(SLOTS, lines_here),
            array(LIST, 128),
            flag,
        ),
        2 * held * n_sep * chips * SLOTS,
        MIB,
        (0,),
    )(me, sep_rows, sep_rhs, sep_update, leaf_rows, arrived)

    mail = array(chips, SLOTS + LIST, wide)
    blocks = kernel_call(select_body, mail, SLOTS * lines_here * wide, MIB, limit=4)(
        select, lines, listed
    )

    def few_rows(blocks, lines, listed, sep_rows):
        return to_all(blocks, XY)

    def all_rows(blocks, lines, listed, sep_rows):
        full = array(chips, lines_here + LIST, wide)
        full = kernel_call(all_lines_body, full, 1024, 2 * MIB)(lines, listed)
        return kernel_call(functools.partial(all_rows_body, sizes), mail, 1024, 2 * MIB)(sep_rows, to_all(full, XY))

    root_rows = lax.cond(fits[0] == 1, few_rows, all_rows, blocks, lines, listed, sep_rows)

    terms = kernel_call(
        terms_body,
        array(chips, wide, sep // chips),
        2 * held * wide * (chips * SLOTS + sep),
        6 * MIB,
        in_hbm=(3, 4),
        scratch=(
            pltpu.VMEM(sep_inv_cols.shape, BF16),
            pltpu.VMEM(sep_inv_cols.shape, BF16),
            pltpu.SemaphoreType.DMA((2,)),
        ),
    )(rhs, spread, root_rows, sep_inv_cols, other_inverse)
    terms = to_all(terms, XY)

    select, place, fits = kernel_call(
        functools.partial(leaf_plan_body, sizes, sep, held),
        (
            array(chips, SLOTS, held + lines_here),
            array(cores * n_leaf, 1, dtype=I32),
            flag,
        ),
        chips * 2**26,
        2 * MIB,
        (0,),
        scratch=(
            pltpu.VMEM((chips, cores * n_leaf), I32),
            pltpu.VMEM((chips, cores * n_leaf), I32),
        ),
    )(me, root_rows)
    mail = array(chips, SLOTS, wide)
    value, blocks = kernel_call(
        sum_body, (array(held, wide), mail), 2 * chips * SLOTS * wide * (held + lines_here), 2 * MIB
    )(terms, select, lines)

    def few_ancestors(blocks, value, lines, listed):
        return to_all(blocks, XY)

    def all_ancestors(blocks, value, lines, listed):
        table = jnp.concatenate([value, lines], axis=0)
        table = to_all(jnp.broadcast_to(table, (chips, *table.shape)), XY)
        return kernel_call(functools.partial(all_ancestors_body, sizes, sep, held), mail, 1024, 2 * MIB)(listed, table)

    ancestors = lax.cond(fits[0] == 1, few_ancestors, all_ancestors, blocks, value, lines, listed)

    own_rows, sent = kernel_call(
        ancestors_body,
        (array(n_leaf, wide), array(n_leaf + own_sep, wide)),
        2 * cores * n_leaf * wide * chips * SLOTS,
        MIB,
        (0,),
    )(me, place, ancestors, value)
    arrived = swapped(sent)
    leaf_out, sep_out = kernel_call(
        leaf_body,
        (array(*leaf_rhs.shape), array(own_sep, nrhs)),
        2 * nrhs * (leaf_inv.size + leaf_update.size),
        4 * MIB,
        (0, 1),
        limit=62.8,
        in_hbm=(5, 6, 7),
        scratch=(
            pltpu.VMEM(leaf_rhs.shape, BF16),
            pltpu.VMEM(leaf_update.shape, BF16),
            pltpu.VMEM(leaf_inv.shape, BF16),
            pltpu.SemaphoreType.DMA((3,)),
        ),
    )(me, leaf_cols, own_rows, arrived, value, leaf_rhs, leaf_update, leaf_inv)
    return (sep_out, leaf_out)


def solution(mesh):
    finer = Mesh(mesh.devices.reshape(mesh.shape["grp"], 4, 4, 2), ALL)
    split = P(ALL, None)
    in_specs = (split, split, split, P("grp", None), split, split, split, split, P(ALL), split)
    return jax.shard_map(
        on_device, mesh=finer, in_specs=in_specs, out_specs=(split, split), check_vma=False
    )
```

time: 113 us -> 94.8 us (0.84)
  waiting for transfers between devices: 28.8 us -> 10.8 us
  starting transfers between devices: 45.9 us -> 29.7 us
  blocking collectives: 18.8 us -> 26.7 us
  Pallas kernels: 13.2 us -> 17.4 us
  local copies, waits for them, and re-layouts: 4.42 us -> 6.77 us
  between operations: 1.47 us -> 2.71 us
    all_to_all x3 -> x2, waiting for transfers between devices: 26.5 us -> 9.37 us  [to_all(): return lax.all_to_all(blocks, axes, 0, 0, tiled=True)]
    all_to_all x3 -> x2, starting transfers between devices: 27.1 us -> 13.7 us  [to_all(): return lax.all_to_all(blocks, axes, 0, 0, tiled=True)]
    all_to_all x1 -> x2, blocking collectives: 18.8 us -> 26.7 us  [to_all(): return lax.all_to_all(blocks, axes, 0, 0, tiled=True)]
    unnamed x14 -> x22, local copies, waits for them, and re-layouts: 1.86 us -> 6.77 us
    pallas_call x8 -> x9, Pallas kernels: 13.2 us -> 17.4 us  [call(): pl.pallas_call(body, out_shape=outs, in_specs=specs, out_specs=jax.tree.m...]
    ppermute x5 -> x3, starting transfers between devices: 18.7 us -> 16 us  [swapped(): return lax.ppermute(value, CORE, [(0, 1), (1, 0)])]
    broadcast_in_dim x2 -> x0, local copies, waits for them, and re-layouts: 2.55 us -> none  [the longest x1 1.37 us: on_device(): blocks = jnp.broadcast_to(blocks, (groups, cores, own_root, wide))]
    ppermute x5 -> x3, waiting for transfers between devices: 2.33 us -> 1.43 us  [swapped(): return lax.ppermute(value, CORE, [(0, 1), (1, 0)])]
  transfers between devices with their start and end apart: 8 -> 5, of which waited for: 6 -> 4; matrix products, arithmetic and copies ran while one was open for 1% -> 0% of each run, Pallas kernels for 3% -> 10%
where the time goes in v3:
time: 94.8 us; the launch traced here: 94.2 us
  starting transfers between devices  29.7 us (31%)
  blocking collectives  26.7 us (28%)
  Pallas kernels  17.4 us (18%)
  waiting for transfers between devices  10.8 us (11%)
  local copies, waits for them, and re-layouts  6.77 us (7%)
  between operations  2.71 us (3%)
    all_to_all x2, blocking collectives, to_all(): return lax.all_to_all(blocks, axes, 0, 0, tiled=True)  26.7 us
    pallas_call x9, Pallas kernels, call(): pl.pallas_call(body, out_shape=outs, in_specs=specs, out_specs=jax.tree.m...  17.4 us
    ppermute x3, starting transfers between devices, swapped(): return lax.ppermute(value, CORE, [(0, 1), (1, 0)])  16 us
    all_to_all x2, starting transfers between devices, to_all(): return lax.all_to_all(blocks, axes, 0, 0, tiled=True)  13.7 us
    all_to_all x2, waiting for transfers between devices, to_all(): return lax.all_to_all(blocks, axes, 0, 0, tiled=True)  9.37 us
    unnamed x22, local copies, waits for them, and re-layouts  6.77 us
  transfers between devices with their start and end apart: 5, of which 4 were waited for; matrix products, arithmetic and copies ran while one was open for 0% of the time, Pallas kernels for 10%

profile of v3, /device:TPU:1, one launch (start us, length us, event | category | flops | bytes accessed | tf_op | source)
XLA Modules:
  0.0 94.2 jit_solution(399339186582555966)
XLA Ops:
  0.6 8.7 %collective-permute-start.1 = (bf16[128,4096]{1,0:T(8,128)(2,1)}, bf16[128,4096]{1,0:T(8,128)(2,1)S(1)}, u32[]{:S(2)}, u32[]{:S(2)}) collective-permute-start(bf16[128,4096]{1,0:T(8,128)(2,1)} %own_inverse_at.1), channel_id=1, source_target_pairs={{0,1},{1,0},{2,3},{3,2},{4,5},{5,4},{6,7},{7,6},{8,9},{9,8},{10,11... | collective-permute-start | bytes 3145736 | tf_op jit(solution)/shard_map/ppermute | solution.py:25
  9.4 0.7 copy-done.7
  10.7 10.0 %all-to-all-start.4 = ((bf16[32,8,128]{2,1,0:T(8,128)(2,1)}), bf16[32,8,128]{2,1,0:T(8,128)(2,1)S(1)}, u32[]{:S(2)}, u32[]{:S(2)}) async-start(bf16[32,8,128]{2,1,0:T(8,128)(2,1)} %shard_map.115), calls=%async_computation.4 | async-start | bytes 131072 | tf_op jit(solution)/shard_map/all_to_all | solution.py:21
  20.8 0.9 copy-done.1
  21.7 0.8 copy-done.4
  22.6 0.7 copy-done.8
  23.8 2.1 %collective-permute-start = (bf16[136,640]{1,0:T(8,128)(2,1)S(1)}, bf16[136,640]{1,0:T(8,128)(2,1)S(1)}, u32[]{:S(2)}, u32[]{:S(2)}) collective-permute-start(bf16[136,640]{1,0:T(8,128)(2,1)S(1)} %shard_map.113), channel_id=1, source_target_pairs={{0,1},{1,0},{2,3},{3,2},{4,5},{5,4},{6,7},{7,6},{8,9},{9,8},{10,11... | collective-permute-start | bytes 522248 | tf_op jit(solution)/shard_map/ppermute | solution.py:25
  26.0 1.2 %collective-permute-done.arrived = bf16[136,640]{1,0:T(8,128)(2,1)S(1)} collective-permute-done((bf16[136,640]{1,0:T(8,128)(2,1)S(1)}, bf16[136,640]{1,0:T(8,128)(2,1)S(1)}, u32[]{:S(2)}, u32[]{:S(2)}) %collective-permute-start) | collective-permute-done | bytes 174112 | tf_op jit(solution)/shard_map/ppermute | solution.py:25
  27.1 0.9 copy-done.2
  28.0 0.8 copy-done.5
  28.9 0.7 copy-done.9
  29.5 1.7 %shard_map.114 = (bf16[256,128]{1,0:T(8,128)(2,1)S(1)}, bf16[256,1024]{1,0:T(8,128)(2,1)S(1)}, bf16[64,256]{1,0:T(8,128)(2,1)S(1)}, bf16[8,128]{1,0:T(8,128)(2,1)S(1)}, s32[1]{0:T(128)}) custom-call(s32[2]{0:T(128)S(1)} %pad_add_fusion.core.me, s32[1,512]{1,0:T(1,128)} %rows.1, bf16[128,256]{1,0:T(8,128)(2,1)S(1)} %copy-done.5, ...), custom_call_target="tpu_custom_call" | custom-call | flops 268435456 | bytes 1048576 | tf_op jit(solution)/shard_map/pallas_call | solution.py:57
  31.9 1.8 %all-to-all-done.4 = bf16[32,8,128]{2,1,0:T(8,128)(2,1)S(1)} async-done(((bf16[32,8,128]{2,1,0:T(8,128)(2,1)}), bf16[32,8,128]{2,1,0:T(8,128)(2,1)S(1)}, u32[]{:S(2)}, u32[]{:S(2)}) %all-to-all-start.4) | async-done | bytes 65568 | tf_op jit(solution)/shard_map/all_to_all | solution.py:21
  33.9 14.2 %conditional.2 = (bf16[16,72,128]{2,1,0:T(8,128)(2,1)S(1)}) conditional(s32[]{:T(128)} %bitcast.2, (bf16[256,128]{1,0:T(8,128)(2,1)S(1)}, bf16[8,128]{1,0:T(8,128)(2,1)S(1)}, s32[1,512]{1,0:T(1,128)}) %tuple.27, bf16[16,72,128]{2,1,0:T(8,128)(2,1)S(1)} %shard_map.116), branch_computations={%region_0.0_spmd, %region_1.0_spmd} | conditional | flops 2048 | bytes 6365220 | solution.py:395
  33.9 14.2 %all_to_all.27 = bf16[16,72,128]{2,1,0:T(8,128)(2,1)S(1)} all-to-all(bf16[16,72,128]{2,1,0:T(8,128)(2,1)S(1)} %param.1), channel_id=1, replica_groups=mesh['grp'=16,'dev_0'=4,'dev_1'=4,'dev_2'=2] {'dev_0','dev_1'}, dimensions={0} | all-to-all | bytes 589824 | tf_op jit(solution)/shard_map/cond/branch_1_fun/all_to_all | solution.py:21
  48.1 2.0 %shard_map.118 = bf16[16,128,256]{2,1,0:T(8,128)(2,1)} custom-call(bf16[256,128]{1,0:T(8,128)(2,1)S(1)} %get-tuple-element.47.rhs, bf16[256,1024]{1,0:T(8,128)(2,1)S(1)} %get-tuple-element.48.spread, bf16[16,72,128]{2,1,0:T(8,128)(2,1)S(1)} %get-tuple-element.56.arrived, bf16[128,4096]{1,0:T(8,128)(2,1)S(1)} %copy-done, ...), custom_call_target="tpu_custom_call" | custom-call | flops 335544320 | bytes 6291456 | tf_op jit(solution)/shard_map/pallas_call | solution.py:57
  50.1 3.7 %all-to-all-start.5 = ((bf16[16,128,256]{2,1,0:T(8,128)(2,1)}), bf16[16,128,256]{2,1,0:T(8,128)(2,1)S(1)}, u32[]{:S(2)}, u32[]{:S(2)}) async-start(bf16[16,128,256]{2,1,0:T(8,128)(2,1)} %shard_map.118), calls=%async_computation.5 | async-start | bytes 2097152 | tf_op jit(solution)/shard_map/all_to_all | solution.py:21
  53.8 6.1 %shard_map.117 = (bf16[16,64,512]{2,1,0:T(8,128)(2,1)S(1)}, s32[512,1]{1,0:T(8,128)S(1)}, s32[1]{0:T(128)}) custom-call(s32[2]{0:T(128)S(1)} %pad_add_fusion.core.me, bf16[16,72,128]{2,1,0:T(8,128)(2,1)S(1)} %get-tuple-element.56.arrived), custom_call_target="tpu_custom_call" | custom-call | flops 1073741824 | bytes 2097152 | tf_op jit(solution)/shard_map/pallas_call | solution.py:57
  60.6 7.6 %all-to-all-done.5.terms = bf16[16,128,256]{2,1,0:T(8,128)(2,1)S(1)} async-done(((bf16[16,128,256]{2,1,0:T(8,128)(2,1)}), bf16[16,128,256]{2,1,0:T(8,128)(2,1)S(1)}, u32[]{:S(2)}, u32[]{:S(2)}) %all-to-all-start.5) | async-done | bytes 1048608 | tf_op jit(solution)/shard_map/all_to_all | solution.py:21
  68.7 12.5 %conditional.3 = (bf16[16,64,128]{2,1,0:T(8,128)(2,1)S(1)}) conditional(s32[]{:T(128)} %bitcast.4, (bf16[256,128]{1,0:T(8,128)(2,1)S(1)}, bf16[256,128]{1,0:T(8,128)(2,1)S(1)}, bf16[8,128]{1,0:T(8,128)(2,1)S(1)}) %tuple.28, bf16[16,64,128]{2,1,0:T(8,128)(2,1)S(1)} %get-tuple-element.51), branch_computations={%region_2.0_spmd, %region_3.0_spmd} | conditional | flops 263168 | bytes 8781832 | solution.py:439
  68.7 12.5 %all_to_all.29 = bf16[16,64,128]{2,1,0:T(8,128)(2,1)S(1)} all-to-all(bf16[16,64,128]{2,1,0:T(8,128)(2,1)S(1)} %param.3), channel_id=1, replica_groups=mesh['grp'=16,'dev_0'=4,'dev_1'=4,'dev_2'=2] {'dev_0','dev_1'}, dimensions={0} | all-to-all | bytes 524288 | tf_op jit(solution)/shard_map/cond/branch_1_fun/all_to_all | solution.py:21
  81.2 1.1 %shard_map.120 = (bf16[256,128]{1,0:T(8,128)(2,1)S(1)}, bf16[384,128]{1,0:T(8,128)(2,1)S(1)}) custom-call(s32[2]{0:T(128)S(1)} %pad_add_fusion.core.me, s32[512,1]{1,0:T(8,128)S(1)} %get-tuple-element.45.place, bf16[16,64,128]{2,1,0:T(8,128)(2,1)S(1)} %get-tuple-element.57.arrived, bf16[256,128]{1,0:T(8,128)(2,1)S(1)} %get-tuple-element.50.value), custom_call_target="tpu_custom_call" | custom-call | flops 134217728 | bytes 1048576 | tf_op jit(solution)/shard_map/pallas_call | solution.py:57
  83.0 5.1 %collective-permute-start.2 = (bf16[384,128]{1,0:T(8,128)(2,1)S(1)}, bf16[384,128]{1,0:T(8,128)(2,1)S(1)}, u32[]{:S(2)}, u32[]{:S(2)}) collective-permute-start(bf16[384,128]{1,0:T(8,128)(2,1)S(1)} %get-tuple-element.53), channel_id=1, source_target_pairs={{0,1},{1,0},{2,3},{3,2},{4,5},{5,4},{6,7},{7,6},{8,9},{9,8},{10,11... | collective-permute-start | bytes 294920 | tf_op jit(solution)/shard_map/ppermute | solution.py:25
  89.6 4.5 %shard_map.121 = (bf16[1024,256]{1,0:T(8,128)(2,1)}, bf16[128,256]{1,0:T(8,128)(2,1)}) custom-call(s32[2]{0:T(128)} %copy-done.6, s32[1]{0:T(128)S(6)} %copy.16.cols, bf16[256,128]{1,0:T(8,128)(2,1)} %copy-done.3, bf16[384,128]{1,0:T(8,128)(2,1)} %copy-done.10, bf16[256,128]{1,0:T(8,128)(2,1)S(1)} %get-tuple-element.50.value, bf16[1024,256]{1,0:T(8,128)(2,1)} %rhs_at.1, ...), custom_call_target="tpu_custom_call" | custom-call | flops 671088640 | bytes 4194304 | tf_op jit(solution)/shard_map/pallas_call | solution.py:57
  (22 shorter events, 3.6 us)
Async XLA Ops:
  0.6 47.5 %collective-permute-start.1 = (bf16[128,4096]{1,0:T(8,128)(2,1)}, bf16[128,4096]{1,0:T(8,128)(2,1)S(1)}, u32[]{:S(2)}, u32[]{:S(2)}) collective-permute-start(bf16[128,4096]{1,0:T(8,128)(2,1)} %own_inverse_at.1), channel_id=1, source_target_pairs={{0,1},{1,0},{2,3},{3,2},{4,5},{5,4},{6,7},{7,6},{8,9},{9,8},{10,11... | collective-permute-start | bytes 3145736 | tf_op jit(solution)/shard_map/ppermute | solution.py:25
  9.4 0.7 copy-start.7
  10.7 23.0 %all-to-all-start.4 = ((bf16[32,8,128]{2,1,0:T(8,128)(2,1)}), bf16[32,8,128]{2,1,0:T(8,128)(2,1)S(1)}, u32[]{:S(2)}, u32[]{:S(2)}) async-start(bf16[32,8,128]{2,1,0:T(8,128)(2,1)} %shard_map.115), calls=%async_computation.4 | async-start | bytes 131072 | tf_op jit(solution)/shard_map/all_to_all | solution.py:21
  20.8 0.9 copy-start.1
  21.7 0.8 copy-start.4
  22.6 0.7 copy-start.8
  23.2 58.0 %copy-start.6 = (s32[2]{0:T(128)}, s32[2]{0:T(128)S(1)}, u32[]{:S(2)}) copy-start(s32[2]{0:T(128)S(1)} %pad_add_fusion.core.me) | copy-start | bytes 28
  23.8 3.3 %collective-permute-start = (bf16[136,640]{1,0:T(8,128)(2,1)S(1)}, bf16[136,640]{1,0:T(8,128)(2,1)S(1)}, u32[]{:S(2)}, u32[]{:S(2)}) collective-permute-start(bf16[136,640]{1,0:T(8,128)(2,1)S(1)} %shard_map.113), channel_id=1, source_target_pairs={{0,1},{1,0},{2,3},{3,2},{4,5},{5,4},{6,7},{7,6},{8,9},{9,8},{10,11... | collective-permute-start | bytes 522248 | tf_op jit(solution)/shard_map/ppermute | solution.py:25
  27.1 0.9 copy-start.2
  28.0 0.8 copy-start.5
  28.9 0.7 copy-start.9
  33.9 14.2 %copy-start = (bf16[128,4096]{1,0:T(8,128)(2,1)S(1)}, bf16[128,4096]{1,0:T(8,128)(2,1)}, u32[]{:S(2)}) copy-start(bf16[128,4096]{1,0:T(8,128)(2,1)} %own_inverse_at.1) | copy-start | bytes 3145732
  50.1 18.0 %all-to-all-start.5 = ((bf16[16,128,256]{2,1,0:T(8,128)(2,1)}), bf16[16,128,256]{2,1,0:T(8,128)(2,1)S(1)}, u32[]{:S(2)}, u32[]{:S(2)}) async-start(bf16[16,128,256]{2,1,0:T(8,128)(2,1)} %shard_map.118), calls=%async_computation.5 | async-start | bytes 2097152 | tf_op jit(solution)/shard_map/all_to_all | solution.py:21
  82.3 0.6 copy-start.3
  83.0 6.0 %collective-permute-start.2 = (bf16[384,128]{1,0:T(8,128)(2,1)S(1)}, bf16[384,128]{1,0:T(8,128)(2,1)S(1)}, u32[]{:S(2)}, u32[]{:S(2)}) collective-permute-start(bf16[384,128]{1,0:T(8,128)(2,1)S(1)} %get-tuple-element.53), channel_id=1, source_target_pairs={{0,1},{1,0},{2,3},{3,2},{4,5},{5,4},{6,7},{7,6},{8,9},{9,8},{10,11... | collective-permute-start | bytes 294920 | tf_op jit(solution)/shard_map/ppermute | solution.py:25
  89.0 0.6 copy-start.10

commit v4 on v3

--- a/solution.py
+++ b/solution.py
@@ -8,11 +8,11 @@
 from jax.sharding import Mesh
 from jax.sharding import PartitionSpec as P
 
-ALL = ("grp", "dev_0", "dev_1", "dev_2")
-XY = ("dev_0", "dev_1")
+ALL = ("grp", "x_1", "x_0", "y_1", "y_0", "core")
+XY = ("y_0", "x_0", "y_1", "x_1")
 SLOTS, LIST = 64, 8
 BASE = 64
-CORE = "dev_2"
+CORE = "core"
 BF16, F32, I32 = jnp.bfloat16, jnp.float32, jnp.int32
 MIB = 1 << 20
 
@@ -46,7 +46,7 @@
     return jnp.where(at == places, F32(1.0), F32(0.0)).astype(BF16)
 
 
-def kernel_call(body, outs, flops, n_bytes, in_smem=(), limit=16, in_hbm=(), scratch=()):
+def kernel_call(body, outs, flops, n_bytes, in_smem=(), limit=16, in_hbm=(), out_hbm=(), scratch=()):
     def call(*args):
         specs = [
             pl.BlockSpec(
@@ -58,11 +58,18 @@
             body,
             out_shape=outs,
             in_specs=specs,
-            out_specs=jax.tree.map(
-                lambda out: pl.BlockSpec(
-                    memory_space=pltpu.SMEM if out.ndim == 1 else pltpu.VMEM
-                ),
-                outs,
+            out_specs=jax.tree.unflatten(
+                jax.tree.structure(outs),
+                [
+                    pl.BlockSpec(
+                        memory_space=pltpu.SMEM
+                        if out.ndim == 1
+                        else pltpu.HBM
+                        if i in out_hbm
+                        else pltpu.VMEM
+                    )
+                    for i, out in enumerate(jax.tree.leaves(outs))
+                ],
             ),
             scratch_shapes=scratch,
             cost_estimate=pl.CostEstimate(
@@ -79,16 +86,22 @@
     return size.bit_length() - 1
 
 
+def spot(chip):
+    bits = [(chip >> i) & 1 for i in range(4)]
+    return (bits[0] << 3) + (bits[2] << 2) + (bits[1] << 1) + bits[3]
+
+
 def root_owner(rows, own, cores, devices, groups):
     device = (rows >> log2(own)) & (devices - 1)
-    line = ((rows >> log2(own * devices)) << log2(cores)) + (device & (cores - 1))
-    return device >> log2(cores), (line << log2(own)) + (rows & (own - 1))
+    group = rows >> log2(own * devices)
+    line = ((device & (cores - 1)) << log2(groups)) + group
+    return spot(device >> log2(cores)), (line << log2(own)) + (rows & (own - 1))
 
 
 def ancestor_owner(sizes, sep, held, rows):
     chip, line = root_owner(rows - sep, *sizes)
     here = rows < sep
-    return jnp.where(here, rows >> log2(held), chip), jnp.where(here, rows & (held - 1), held + line)
+    return jnp.where(here, spot(rows >> log2(held)), chip), jnp.where(here, rows & (held - 1), held + line)
 
 
 def before(size):
@@ -133,9 +146,10 @@
 def fan_body(root, out):
     half = root.shape[1] // 2
     low, high = root[:, :half], root[:, half:]
-    for i in range(0, out.shape[0], 2):
+    groups = out.shape[0] // 2
+    for i in range(groups):
         out[i] = low
-        out[i + 1] = high
+        out[groups + i] = high
 
 
 def pack_body(core, rhs, update, leaf_rows, out):
@@ -206,11 +220,14 @@
     picked = dot(chosen(owner * held + line, chips * held), table).astype(BF16)
     full = picked.shape[0] // SLOTS
     out[:full, :SLOTS] = picked.reshape(full, SLOTS, wide)
-    out[full:, :SLOTS] = jnp.zeros((chips - full, SLOTS, wide), BF16)
+    if chips > full:
+        out[full:, :SLOTS] = jnp.zeros((chips - full, SLOTS, wide), BF16)
     out[:, SLOTS:] = arrived[:, held:]
 
 
-def terms_body(rhs, spread, arrived, own_inverse_at, other_inverse_at, out, own_inverse, other_inverse, sems):
+def terms_body(
+    rhs, spread, arrived, own_inverse_at, other_inverse_at, out, own_inverse, other_inverse, block, sems
+):
     copies = (
         pltpu.make_async_copy(own_inverse_at, own_inverse, sems.at[0]),
         pltpu.make_async_copy(other_inverse_at, other_inverse, sems.at[1]),
@@ -224,10 +241,16 @@
     residual = residual.astype(BF16).astype(F32).T.astype(BF16)
     for copy in copies:
         copy.wait()
-    for i in range(chips):
-        at = slice(i * width, (i + 1) * width)
+    sent = []
+    for chip in range(chips):
+        i = spot(chip)
+        at = slice(chip * width, (chip + 1) * width)
         both = jnp.concatenate([own_inverse[:, at], other_inverse[:, at]], axis=0)
-        out[i] = dot(residual, both).astype(BF16)
+        block[i] = dot(residual, both).astype(BF16)
+        sent.append(pltpu.make_async_copy(block.at[i], out.at[i], sems.at[2 + i]))
+        sent[-1].start()
+    for copy in sent:
+        copy.wait()
 
 
 def leaf_plan_body(sizes, sep, held, me, arrived, select_out, place_out, fits_out, mine_at, line_at):
@@ -287,7 +310,8 @@
         total = total + dot(chosen(place - i * lines, lines), arrived[i])
     full = total.shape[0] // SLOTS
     out[:full] = total.astype(BF16).reshape(full, SLOTS, wide)
-    out[full:] = jnp.zeros((chips - full, SLOTS, wide), BF16)
+    if chips > full:
+        out[full:] = jnp.zeros((chips - full, SLOTS, wide), BF16)
 
 
 def ancestors_body(me, place, arrived, value, own, sent):
@@ -300,28 +324,24 @@
     sent[half:] = of_core(me[0] != 0, value[...])
 
 
-def leaf_body(
-    me, cols, own, arrived, value, rhs_at, update_at, inverse_at, out, sep_out, rhs, update, inverse, sems
-):
-    fetches = [
-        pltpu.make_async_copy(source, target, sems.at[i])
-        for i, (source, target) in enumerate(
-            ((update_at, update), (rhs_at, rhs), (inverse_at, inverse))
-        )
-    ]
-    for fetch in fetches:
-        fetch.start()
+def leaf_body(me, cols, own, arrived, value, rhs, update, inverse, out, sep_out, block, sems):
     first, half = me[0] == 0, own.shape[0]
     rows = joined(first, own[...], arrived[:half])
+    live = lax.broadcasted_iota(I32, out.shape, 0) < cols[0]
+    residual = rhs[...].astype(F32) - dot(update[...], rows)
+    residual = jnp.where(live, residual, F32(0.0)).astype(BF16)
+    size = out.shape[0] // sems.shape[0]
+    sent = []
+    for i in range(sems.shape[0]):
+        at = pl.ds(i * size, size)
+        solved = dot(inverse[at, :], residual)
+        live = lax.broadcasted_iota(I32, solved.shape, 0) < cols[0] - i * size
+        block[at, :] = jnp.where(live, solved, F32(0.0)).astype(BF16)
+        sent.append(pltpu.make_async_copy(block.at[at], out.at[at], sems.at[i]))
+        sent[-1].start()
     sep_out[...] = joined(first, of_core(first, value[...]), arrived[half:])
-    live = lax.broadcasted_iota(I32, out.shape, 0) < cols[0]
-    fetches[0].wait()
-    term = dot(update[...], rows)
-    fetches[1].wait()
-    residual = jnp.where(live, rhs[...].astype(F32) - term, F32(0.0)).astype(BF16)
-    fetches[2].wait()
-    solved = dot(inverse[...], residual)
-    out[...] = jnp.where(live, solved, F32(0.0)).astype(BF16)
+    for copy in sent:
+        copy.wait()
 
 
 def on_device(
@@ -357,7 +377,7 @@
     blocks = kernel_call(fan_body, array(groups * cores, own_root, wide), 1024, MIB, limit=4)(
         root_solution
     )
-    lines = to_all(blocks, ("grp", CORE)).reshape(lines_here, wide)
+    lines = to_all(blocks, (CORE, "grp")).reshape(lines_here, wide)
 
     other_inverse = swapped(sep_inv_cols)
     sent = kernel_call(
@@ -400,10 +420,12 @@
         2 * held * wide * (chips * SLOTS + sep),
         6 * MIB,
         in_hbm=(3, 4),
+        out_hbm=(0,),
         scratch=(
             pltpu.VMEM(sep_inv_cols.shape, BF16),
             pltpu.VMEM(sep_inv_cols.shape, BF16),
-            pltpu.SemaphoreType.DMA((2,)),
+            pltpu.VMEM((chips, wide, sep // chips), BF16),
+            pltpu.SemaphoreType.DMA((2 + chips,)),
         ),
     )(rhs, spread, root_rows, sep_inv_cols, other_inverse)
     terms = to_all(terms, XY)
@@ -452,20 +474,14 @@
         2 * nrhs * (leaf_inv.size + leaf_update.size),
         4 * MIB,
         (0, 1),
-        limit=62.8,
-        in_hbm=(5, 6, 7),
-        scratch=(
-            pltpu.VMEM(leaf_rhs.shape, BF16),
-            pltpu.VMEM(leaf_update.shape, BF16),
-            pltpu.VMEM(leaf_inv.shape, BF16),
-            pltpu.SemaphoreType.DMA((3,)),
-        ),
+        out_hbm=(0,),
+        scratch=(pltpu.VMEM(leaf_rhs.shape, BF16), pltpu.SemaphoreType.DMA((4,))),
     )(me, leaf_cols, own_rows, arrived, value, leaf_rhs, leaf_update, leaf_inv)
     return (sep_out, leaf_out)
 
 
 def solution(mesh):
-    finer = Mesh(mesh.devices.reshape(mesh.shape["grp"], 4, 4, 2), ALL)
+    finer = Mesh(mesh.devices.reshape(mesh.shape["grp"], 2, 2, 2, 2, 2), ALL)
     split = P(ALL, None)
     in_specs = (split, split, split, P("grp", None), split, split, split, split, P(ALL), split)
     return jax.shard_map(

time: 94.8 us -> 95.1 us (level)
  blocking collectives: 26.7 us -> 28.2 us
  local copies, waits for them, and re-layouts: 6.77 us -> 5.54 us
  waiting for transfers between devices: 10.8 us -> 12 us
    all_to_all x2, blocking collectives: 26.7 us -> 28.2 us  [to_all(): return lax.all_to_all(blocks, axes, 0, 0, tiled=True)]
    unnamed x22, local copies, waits for them, and re-layouts: 6.77 us -> 5.54 us
    all_to_all x2, waiting for transfers between devices: 9.37 us -> 10.6 us  [to_all(): return lax.all_to_all(blocks, axes, 0, 0, tiled=True)]
where the time goes in v4:
time: 95.1 us; the launch traced here: 94.4 us
  starting transfers between devices  29 us (30%)
  blocking collectives  28.2 us (30%)
  Pallas kernels  16.8 us (18%)
  waiting for transfers between devices  12 us (13%)
  local copies, waits for them, and re-layouts  5.54 us (6%)
  between operations  2.7 us (3%)
    all_to_all x2, blocking collectives, to_all(): return lax.all_to_all(blocks, axes, 0, 0, tiled=True)  28.2 us
    pallas_call x9, Pallas kernels, call(): pl.pallas_call(body, out_shape=outs, in_specs=specs, out_specs=jax.tree.u...  16.8 us
    ppermute x3, starting transfers between devices, swapped(): return lax.ppermute(value, CORE, [(0, 1), (1, 0)])  15.3 us
    all_to_all x2, starting transfers between devices, to_all(): return lax.all_to_all(blocks, axes, 0, 0, tiled=True)  13.7 us
    all_to_all x2, waiting for transfers between devices, to_all(): return lax.all_to_all(blocks, axes, 0, 0, tiled=True)  10.6 us
    unnamed x22, local copies, waits for them, and re-layouts  5.54 us
  transfers between devices with their start and end apart: 5, of which 4 were waited for; matrix products, arithmetic and copies ran while one was open for 0% of the time, Pallas kernels for 10%

profile of v4, /device:TPU:1, one launch (start us, length us, event | category | flops | bytes accessed | tf_op | source)
XLA Modules:
  0.0 94.4 jit_solution(1900245793142655336)
XLA Ops:
  0.6 8.7 %collective-permute-start.1 = (bf16[128,4096]{1,0:T(8,128)(2,1)}, bf16[128,4096]{1,0:T(8,128)(2,1)S(1)}, u32[]{:S(2)}, u32[]{:S(2)}) collective-permute-start(bf16[128,4096]{1,0:T(8,128)(2,1)} %own_inverse_at.1), channel_id=1, source_target_pairs={{0,1},{1,0},{2,3},{3,2},{4,5},{5,4},{6,7},{7,6},{8,9},{9,8},{10,11... | collective-permute-start | bytes 3145736 | tf_op jit(solution)/shard_map/ppermute | solution.py:25
  9.4 0.7 copy-done.8
  10.7 10.0 %all-to-all-start.4 = ((bf16[32,8,128]{2,1,0:T(8,128)(2,1)}), bf16[32,8,128]{2,1,0:T(8,128)(2,1)S(1)}, u32[]{:S(2)}, u32[]{:S(2)}) async-start(bf16[32,8,128]{2,1,0:T(8,128)(2,1)} %shard_map.115), calls=%async_computation.4 | async-start | bytes 131072 | tf_op jit(solution)/shard_map/all_to_all | solution.py:21
  20.8 0.9 copy-done.4
  21.7 0.8 copy-done.6
  22.6 0.7 copy-done.9
  23.8 2.1 %collective-permute-start = (bf16[136,640]{1,0:T(8,128)(2,1)S(1)}, bf16[136,640]{1,0:T(8,128)(2,1)S(1)}, u32[]{:S(2)}, u32[]{:S(2)}) collective-permute-start(bf16[136,640]{1,0:T(8,128)(2,1)S(1)} %shard_map.113), channel_id=1, source_target_pairs={{0,1},{1,0},{2,3},{3,2},{4,5},{5,4},{6,7},{7,6},{8,9},{9,8},{10,11... | collective-permute-start | bytes 522248 | tf_op jit(solution)/shard_map/ppermute | solution.py:25
  26.0 1.2 %collective-permute-done.arrived = bf16[136,640]{1,0:T(8,128)(2,1)S(1)} collective-permute-done((bf16[136,640]{1,0:T(8,128)(2,1)S(1)}, bf16[136,640]{1,0:T(8,128)(2,1)S(1)}, u32[]{:S(2)}, u32[]{:S(2)}) %collective-permute-start) | collective-permute-done | bytes 174112 | tf_op jit(solution)/shard_map/ppermute | solution.py:25
  27.1 0.9 copy-done.5
  28.0 0.8 copy-done.7
  29.5 1.7 %shard_map.114 = (bf16[256,128]{1,0:T(8,128)(2,1)S(1)}, bf16[256,1024]{1,0:T(8,128)(2,1)S(1)}, bf16[64,256]{1,0:T(8,128)(2,1)S(1)}, bf16[8,128]{1,0:T(8,128)(2,1)S(1)}, s32[1]{0:T(128)}) custom-call(s32[2]{0:T(128)S(1)} %pad_add_fusion.core.me, s32[1,512]{1,0:T(1,128)} %rows.1, bf16[128,256]{1,0:T(8,128)(2,1)S(1)} %copy-done.7, ...), custom_call_target="tpu_custom_call" | custom-call | flops 268435456 | bytes 1048576 | tf_op jit(solution)/shard_map/pallas_call | solution.py:57
  31.9 2.5 %all-to-all-done.4 = bf16[32,8,128]{2,1,0:T(8,128)(2,1)S(1)} async-done(((bf16[32,8,128]{2,1,0:T(8,128)(2,1)}), bf16[32,8,128]{2,1,0:T(8,128)(2,1)S(1)}, u32[]{:S(2)}, u32[]{:S(2)}) %all-to-all-start.4) | async-done | bytes 65568 | tf_op jit(solution)/shard_map/all_to_all | solution.py:21
  34.6 15.3 %conditional.2 = (bf16[16,72,128]{2,1,0:T(8,128)(2,1)S(1)}) conditional(s32[]{:T(128)} %bitcast.2, (bf16[256,128]{1,0:T(8,128)(2,1)S(1)}, bf16[8,128]{1,0:T(8,128)(2,1)S(1)}, s32[1,512]{1,0:T(1,128)}) %tuple.27, bf16[16,72,128]{2,1,0:T(8,128)(2,1)S(1)} %shard_map.116), branch_computations={%region_0.0_spmd, %region_1.0_spmd} | conditional | flops 2048 | bytes 6365220 | solution.py:415
  34.7 15.2 %all_to_all.27 = bf16[16,72,128]{2,1,0:T(8,128)(2,1)S(1)} all-to-all(bf16[16,72,128]{2,1,0:T(8,128)(2,1)S(1)} %param.1), channel_id=1, replica_groups=mesh['grp'=16,'x_1'=2,'x_0'=2,'y_1'=2,'y_0'=2,'core'=2] {'y_0','x_0','y_..., dimensions={0} | all-to-all | bytes 589824 | tf_op jit(solution)/shard_map/cond/branch_1_fun/all_to_all | solution.py:21
  49.9 1.9 %shard_map.118 = bf16[16,128,256]{2,1,0:T(8,128)(2,1)} custom-call(bf16[256,128]{1,0:T(8,128)(2,1)S(1)} %get-tuple-element.47.rhs, bf16[256,1024]{1,0:T(8,128)(2,1)S(1)} %get-tuple-element.48.spread, bf16[16,72,128]{2,1,0:T(8,128)(2,1)S(1)} %get-tuple-element.56.arrived, bf16[128,4096]{1,0:T(8,128)(2,1)S(1)} %copy-done.1, ...), custom_call_target="tpu_custom_call" | custom-call | flops 335544320 | bytes 6291456 | tf_op jit(solution)/shard_map/pallas_call | solution.py:57
  51.8 3.7 %all-to-all-start.5 = ((bf16[16,128,256]{2,1,0:T(8,128)(2,1)}), bf16[16,128,256]{2,1,0:T(8,128)(2,1)S(1)}, u32[]{:S(2)}, u32[]{:S(2)}) async-start(bf16[16,128,256]{2,1,0:T(8,128)(2,1)} %shard_map.118), calls=%async_computation.5 | async-start | bytes 2097152 | tf_op jit(solution)/shard_map/all_to_all | solution.py:21
  55.5 6.1 %shard_map.117 = (bf16[16,64,512]{2,1,0:T(8,128)(2,1)S(1)}, s32[512,1]{1,0:T(8,128)S(1)}, s32[1]{0:T(128)}) custom-call(s32[2]{0:T(128)S(1)} %pad_add_fusion.core.me, bf16[16,72,128]{2,1,0:T(8,128)(2,1)S(1)} %get-tuple-element.56.arrived), custom_call_target="tpu_custom_call" | custom-call | flops 1073741824 | bytes 2097152 | tf_op jit(solution)/shard_map/pallas_call | solution.py:57
  62.2 8.0 %all-to-all-done.5.terms = bf16[16,128,256]{2,1,0:T(8,128)(2,1)S(1)} async-done(((bf16[16,128,256]{2,1,0:T(8,128)(2,1)}), bf16[16,128,256]{2,1,0:T(8,128)(2,1)S(1)}, u32[]{:S(2)}, u32[]{:S(2)}) %all-to-all-start.5) | async-done | bytes 1048608 | tf_op jit(solution)/shard_map/all_to_all | solution.py:21
  70.3 1.3 %shard_map.119 = (bf16[256,128]{1,0:T(8,128)(2,1)S(1)}, bf16[16,64,128]{2,1,0:T(8,128)(2,1)}) custom-call(bf16[16,128,256]{2,1,0:T(8,128)(2,1)S(1)} %all-to-all-done.5.terms, bf16[16,64,512]{2,1,0:T(8,128)(2,1)S(1)} %get-tuple-element.49.select, bf16[256,128]{1,0:T(8,128)(2,1)S(1)} %bitcast.7), custom_call_target="tpu_custom_call" | custom-call | flops 134217728 | bytes 2097152 | tf_op jit(solution)/shard_map/pallas_call | solution.py:57
  71.6 13.0 %conditional.3 = (bf16[16,64,128]{2,1,0:T(8,128)(2,1)}) conditional(s32[]{:T(128)} %bitcast.4, (bf16[256,128]{1,0:T(8,128)(2,1)S(1)}, bf16[256,128]{1,0:T(8,128)(2,1)S(1)}, bf16[8,128]{1,0:T(8,128)(2,1)S(1)}) %tuple.28, bf16[16,64,128]{2,1,0:T(8,128)(2,1)} %get-tuple-element.51), branch_computations={%region_2.0_spmd, %region_3.0_spmd} | conditional | flops 263168 | bytes 8781832 | solution.py:461
  71.6 13.0 %all_to_all.29 = bf16[16,64,128]{2,1,0:T(8,128)(2,1)} all-to-all(bf16[16,64,128]{2,1,0:T(8,128)(2,1)} %param.3), channel_id=1, replica_groups=mesh['grp'=16,'x_1'=2,'x_0'=2,'y_1'=2,'y_0'=2,'core'=2] {'y_0','x_0','y_..., dimensions={0} | all-to-all | bytes 524288 | tf_op jit(solution)/shard_map/cond/branch_1_fun/all_to_all | solution.py:21
  84.6 1.6 %shard_map.120 = (bf16[256,128]{1,0:T(8,128)(2,1)S(1)}, bf16[384,128]{1,0:T(8,128)(2,1)S(1)}) custom-call(s32[2]{0:T(128)S(1)} %pad_add_fusion.core.me, s32[512,1]{1,0:T(8,128)S(1)} %get-tuple-element.45.place, bf16[16,64,128]{2,1,0:T(8,128)(2,1)} %get-tuple-element.57.arrived, bf16[256,128]{1,0:T(8,128)(2,1)S(1)} %get-tuple-element.50.value), custom_call_target="tpu_custom_call" | custom-call | flops 134217728 | bytes 1048576 | tf_op jit(solution)/shard_map/pallas_call | solution.py:57
  86.1 4.5 %collective-permute-start.2 = (bf16[384,128]{1,0:T(8,128)(2,1)S(1)}, bf16[384,128]{1,0:T(8,128)(2,1)S(1)}, u32[]{:S(2)}, u32[]{:S(2)}) collective-permute-start(bf16[384,128]{1,0:T(8,128)(2,1)S(1)} %get-tuple-element.53), channel_id=1, source_target_pairs={{0,1},{1,0},{2,3},{3,2},{4,5},{5,4},{6,7},{7,6},{8,9},{9,8},{10,11... | collective-permute-start | bytes 294920 | tf_op jit(solution)/shard_map/ppermute | solution.py:25
  91.5 2.8 %shard_map.121 = (bf16[1024,256]{1,0:T(8,128)(2,1)}, bf16[128,256]{1,0:T(8,128)(2,1)}) custom-call(s32[2]{0:T(128)S(1)} %pad_add_fusion.core.me, s32[1]{0:T(128)S(6)} %copy.16.cols, bf16[256,128]{1,0:T(8,128)(2,1)S(1)} %get-tuple-element.52.own, bf16[384,128]{1,0:T(8,128)(2,1)S(1)} %collective-permute-done.2.arrived, ...), custom_call_target="tpu_custom_call" | custom-call | flops 671088640 | bytes 4194304 | tf_op jit(solution)/shard_map/pallas_call | solution.py:57
  (22 shorter events, 2.4 us)
Async XLA Ops:
  0.6 49.3 %collective-permute-start.1 = (bf16[128,4096]{1,0:T(8,128)(2,1)}, bf16[128,4096]{1,0:T(8,128)(2,1)S(1)}, u32[]{:S(2)}, u32[]{:S(2)}) collective-permute-start(bf16[128,4096]{1,0:T(8,128)(2,1)} %own_inverse_at.1), channel_id=1, source_target_pairs={{0,1},{1,0},{2,3},{3,2},{4,5},{5,4},{6,7},{7,6},{8,9},{9,8},{10,11... | collective-permute-start | bytes 3145736 | tf_op jit(solution)/shard_map/ppermute | solution.py:25
  9.4 0.7 copy-start.8
  10.7 23.8 %all-to-all-start.4 = ((bf16[32,8,128]{2,1,0:T(8,128)(2,1)}), bf16[32,8,128]{2,1,0:T(8,128)(2,1)S(1)}, u32[]{:S(2)}, u32[]{:S(2)}) async-start(bf16[32,8,128]{2,1,0:T(8,128)(2,1)} %shard_map.115), calls=%async_computation.4 | async-start | bytes 131072 | tf_op jit(solution)/shard_map/all_to_all | solution.py:21
  20.8 0.9 copy-start.4
  21.7 0.8 copy-start.6
  22.6 0.7 copy-start.9
  23.8 3.3 %collective-permute-start = (bf16[136,640]{1,0:T(8,128)(2,1)S(1)}, bf16[136,640]{1,0:T(8,128)(2,1)S(1)}, u32[]{:S(2)}, u32[]{:S(2)}) collective-permute-start(bf16[136,640]{1,0:T(8,128)(2,1)S(1)} %shard_map.113), channel_id=1, source_target_pairs={{0,1},{1,0},{2,3},{3,2},{4,5},{5,4},{6,7},{7,6},{8,9},{9,8},{10,11... | collective-permute-start | bytes 522248 | tf_op jit(solution)/shard_map/ppermute | solution.py:25
  27.1 0.9 copy-start.5
  28.0 0.8 copy-start.7
  28.9 0.7 copy-start.10
  34.6 15.3 %copy-start.1 = (bf16[128,4096]{1,0:T(8,128)(2,1)S(1)}, bf16[128,4096]{1,0:T(8,128)(2,1)}, u32[]{:S(2)}) copy-start(bf16[128,4096]{1,0:T(8,128)(2,1)} %own_inverse_at.1) | copy-start | bytes 3145732
  51.8 18.5 %all-to-all-start.5 = ((bf16[16,128,256]{2,1,0:T(8,128)(2,1)}), bf16[16,128,256]{2,1,0:T(8,128)(2,1)S(1)}, u32[]{:S(2)}, u32[]{:S(2)}) async-start(bf16[16,128,256]{2,1,0:T(8,128)(2,1)} %shard_map.118), calls=%async_computation.5 | async-start | bytes 2097152 | tf_op jit(solution)/shard_map/all_to_all | solution.py:21
  71.6 20.0 %copy-start = (bf16[1024,1024]{1,0:T(8,128)(2,1)S(1)}, bf16[1024,1024]{1,0:T(8,128)(2,1)}, u32[]{:S(2)}) copy-start(bf16[1024,1024]{1,0:T(8,128)(2,1)} %inverse.1) | copy-start | bytes 6291460
  71.6 20.0 %copy-start.2 = (bf16[1024,256]{1,0:T(8,128)(2,1)S(1)}, bf16[1024,256]{1,0:T(8,128)(2,1)}, u32[]{:S(2)}) copy-start(bf16[1024,256]{1,0:T(8,128)(2,1)} %rhs.5) | copy-start | bytes 1572868
  71.6 20.0 %copy-start.3 = (bf16[1024,256]{1,0:T(8,128)(2,1)S(1)}, bf16[1024,256]{1,0:T(8,128)(2,1)}, u32[]{:S(2)}) copy-start(bf16[1024,256]{1,0:T(8,128)(2,1)} %update.5) | copy-start | bytes 1572868
  86.1 5.4 %collective-permute-start.2 = (bf16[384,128]{1,0:T(8,128)(2,1)S(1)}, bf16[384,128]{1,0:T(8,128)(2,1)S(1)}, u32[]{:S(2)}, u32[]{:S(2)}) collective-permute-start(bf16[384,128]{1,0:T(8,128)(2,1)S(1)} %get-tuple-element.53), channel_id=1, source_target_pairs={{0,1},{1,0},{2,3},{3,2},{4,5},{5,4},{6,7},{7,6},{8,9},{9,8},{10,11... | collective-permute-start | bytes 294920 | tf_op jit(solution)/shard_map/ppermute | solution.py:25

commit v5 on v4

--- a/solution.py
+++ b/solution.py
@@ -72,9 +72,7 @@
                 ],
             ),
             scratch_shapes=scratch,
-            cost_estimate=pl.CostEstimate(
-                flops=flops, bytes_accessed=n_bytes, transcendentals=0
-            ),
+            cost_estimate=pl.CostEstimate(flops=flops, bytes_accessed=n_bytes, transcendentals=0),
             compiler_params=pltpu.CompilerParams(vmem_limit_bytes=int(limit * MIB)),
         )(*args)
 
@@ -152,28 +150,44 @@
         out[groups + i] = high
 
 
-def pack_body(core, rhs, update, leaf_rows, out):
+def pack_body(
+    core, rhs_at, update_at, rows_at, leaf_rows_at, out, kept, rhs, update, wanted, listed, sems
+):
+    pairs = ((rhs_at, rhs), (update_at, update), (rows_at, wanted), (leaf_rows_at, listed))
+    fetches = [pltpu.make_async_copy(*pair, sems.at[i]) for i, pair in enumerate(pairs)]
+    for fetch in fetches:
+        fetch.start()
+    for fetch in fetches:
+        fetch.wait()
     rows, half = rhs.shape[0], rhs.shape[1] // 2
-    out[:rows, :half] = side(core[0] != 0, rhs[...])
-    out[:rows, half:] = update[...]
-    listed = leaf_rows[...]
-    digits = jnp.concatenate([listed >> log2(BASE), listed & (BASE - 1)], axis=1)
-    spare = out.shape[0] - rows
-    digits = jnp.broadcast_to(digits.astype(F32), (spare, digits.shape[1]))
-    out[rows:, : digits.shape[1]] = digits.astype(BF16)
-    out[rows:, digits.shape[1] :] = jnp.zeros((spare, out.shape[1] - digits.shape[1]), BF16)
+    first = core[0] == 0
+    width = update.shape[1]
+    leaf, sep = listed[...], wanted[...]
+    digits = [
+        jnp.concatenate([leaf >> log2(BASE), leaf & (BASE - 1)], axis=1),
+        sep >> log2(BASE),
+        sep & (BASE - 1),
+    ]
+    digits = jnp.concatenate(digits + [jnp.zeros((LIST - 3, width), I32)], axis=0)
+    digits = digits.astype(F32).astype(BF16)
+    for target, take in ((out, jnp.logical_not(first)), (kept, first)):
+        target[:rows, :half] = side(take, rhs[...])
+        target[:rows, half:] = update[...]
+        target[rows:, :half] = jnp.zeros((LIST, half), BF16)
+        target[rows:, half:] = digits
 
 
 def plan_body(
-    sizes, me, rows, rhs, update, leaf_rows, arrived, rhs_out, spread_out, select_out, list_out, fits_out
+    sizes, chip_at, kept, arrived, rhs_out, spread_out, select_out, list_out, fits_out
 ):
-    own, half = rhs.shape[0], rhs.shape[1] // 2
-    core, chip = me[0], me[1]
-    rhs_out[...] = jnp.concatenate([side(core == 0, rhs[...]), arrived[:own, :half]], axis=0)
-    both = jnp.concatenate([update[...], arrived[:own, half:]], axis=0)
+    own, half = kept.shape[0] - LIST, rhs_out.shape[1]
+    chip = chip_at[0]
+    rhs_out[...] = jnp.concatenate([kept[:own, :half], arrived[:own, :half]], axis=0)
+    both = jnp.concatenate([kept[:own, half:], arrived[:own, half:]], axis=0)
+    digits, other_digits = kept[own:, half:].astype(F32), arrived[own:, half:].astype(F32)
 
     chips = spread_out.shape[1] // SLOTS
-    wanted = rows[...]
+    wanted = (digits[1:2] * F32(BASE) + digits[2:3]).astype(I32)
     size = wanted.shape[1]
     owner, line = root_owner(wanted, *sizes)
     owned = lax.broadcasted_iota(I32, (chips, size), 0) == owner
@@ -191,10 +205,11 @@
     source = one(lax.broadcasted_iota(I32, (lines, size), 0) == line)
     select_out[...] = dot(slot, source, ((1,), (1,))).astype(BF16)
 
-    n_leaf = leaf_rows.shape[1]
-    digits = arrived[own:, : 2 * n_leaf].astype(F32)[:1]
-    other = (digits[:, :n_leaf] * F32(BASE) + digits[:, n_leaf:]).astype(I32)
-    list_out[...] = encoded(jnp.concatenate([leaf_rows[...], other], axis=1))
+    listed = []
+    for line in (digits[:1], other_digits[:1]):
+        n_leaf = line.shape[1] // 2
+        listed.append((line[:, :n_leaf] * F32(BASE) + line[:, n_leaf:]).astype(I32))
+    list_out[...] = encoded(jnp.concatenate(listed, axis=1))
 
 
 def select_body(select, lines, listed, out):
@@ -225,9 +240,7 @@
     out[:, SLOTS:] = arrived[:, held:]
 
 
-def terms_body(
-    rhs, spread, arrived, own_inverse_at, other_inverse_at, out, own_inverse, other_inverse, block, sems
-):
+def terms_body(rhs, spread, arrived, own_inverse_at, other_inverse_at, out, own_inverse, other_inverse, sems):
     copies = (
         pltpu.make_async_copy(own_inverse_at, own_inverse, sems.at[0]),
         pltpu.make_async_copy(other_inverse_at, other_inverse, sems.at[1]),
@@ -241,21 +254,15 @@
     residual = residual.astype(BF16).astype(F32).T.astype(BF16)
     for copy in copies:
         copy.wait()
-    sent = []
-    for chip in range(chips):
-        i = spot(chip)
-        at = slice(chip * width, (chip + 1) * width)
+    for i in range(chips):
+        at = slice(i * width, (i + 1) * width)
         both = jnp.concatenate([own_inverse[:, at], other_inverse[:, at]], axis=0)
-        block[i] = dot(residual, both).astype(BF16)
-        sent.append(pltpu.make_async_copy(block.at[i], out.at[i], sems.at[2 + i]))
-        sent[-1].start()
-    for copy in sent:
-        copy.wait()
-
-
-def leaf_plan_body(sizes, sep, held, me, arrived, select_out, place_out, fits_out, mine_at, line_at):
+        out[spot(i)] = dot(residual, both).astype(BF16)
+
+
+def leaf_plan_body(sizes, sep, held, chip_at, arrived, select_out, place_out, fits_out, mine_at, line_at):
     chips = arrived.shape[0]
-    chip = me[1]
+    chip = chip_at[0]
     rows = jnp.concatenate([decoded(arrived[i, SLOTS:]) for i in range(chips)], axis=0)
     size = rows.shape[1]
     owner, line = ancestor_owner(sizes, sep, held, rows)
@@ -273,7 +280,7 @@
     own_owner = jnp.sum(jnp.where(listed, owner.astype(F32), F32(0.0)), axis=0, keepdims=True)
     place = own_owner * F32(SLOTS) + own_rank
     place = jnp.where(fits == 1, place, lax.broadcasted_iota(I32, (1, size), 1).astype(F32))
-    place_out[...] = column(place).astype(I32)
+    place_out[...] = place.astype(I32)
 
     mine = owner == chip
     mine_at[...] = jnp.where(mine, dot(one(mine), counts), F32(-1.0)).astype(I32)
@@ -314,18 +321,26 @@
         out[full:] = jnp.zeros((chips - full, SLOTS, wide), BF16)
 
 
-def ancestors_body(me, place, arrived, value, own, sent):
+def ancestors_body(core, place, arrived, value, rhs_at, update_at, own, sent, rhs, update, sems):
+    fetches = [
+        pltpu.make_async_copy(update_at, update, sems.at[0]),
+        pltpu.make_async_copy(rhs_at, rhs, sems.at[1]),
+    ]
+    for fetch in fetches:
+        fetch.start()
     chips, slots, wide = arrived.shape
     table = arrived[...].reshape(chips * slots, wide)
     rows = dot(chosen(place[...], chips * slots), table).astype(BF16)
     half = rows.shape[0] // 2
     own[...] = rows[:half]
     sent[:half] = rows[half:]
-    sent[half:] = of_core(me[0] != 0, value[...])
-
-
-def leaf_body(me, cols, own, arrived, value, rhs, update, inverse, out, sep_out, block, sems):
-    first, half = me[0] == 0, own.shape[0]
+    sent[half:] = of_core(core[0] != 0, value[...])
+    for fetch in fetches:
+        fetch.wait()
+
+
+def leaf_body(core, cols, own, arrived, value, rhs, update, inverse, out, sep_out, block, sems):
+    first, half = core[0] == 0, own.shape[0]
     rows = joined(first, own[...], arrived[:half])
     live = lax.broadcasted_iota(I32, out.shape, 0) < cols[0]
     residual = rhs[...].astype(F32) - dot(update[...], rows)
@@ -360,7 +375,7 @@
     chips = lax.axis_size(XY)
     cores = lax.axis_size(CORE)
     devices = chips * cores
-    me = jnp.stack([lax.axis_index(CORE), lax.axis_index(XY)]).astype(I32)
+    core, chip = lax.axis_index(CORE).astype(I32)[None], lax.axis_index(XY).astype(I32)[None]
     own_root, nrhs = root_solution.shape
     own_sep, sep = sep_inv_cols.shape
     wide = nrhs // cores
@@ -380,9 +395,23 @@
     lines = to_all(blocks, (CORE, "grp")).reshape(lines_here, wide)
 
     other_inverse = swapped(sep_inv_cols)
-    sent = kernel_call(
-        pack_body, array(own_sep + 8, wide + n_sep), own_sep, MIB, (0,), 4
-    )(me, sep_rhs, sep_update, leaf_rows)
+    assert n_sep == 2 * n_leaf
+    sent, kept = kernel_call(
+        pack_body,
+        (array(own_sep + LIST, wide + n_sep), array(own_sep + LIST, wide + n_sep)),
+        own_sep,
+        MIB,
+        (0,),
+        63.25,
+        in_hbm=(1, 2, 3, 4),
+        scratch=(
+            pltpu.VMEM(sep_rhs.shape, BF16),
+            pltpu.VMEM(sep_update.shape, BF16),
+            pltpu.VMEM(sep_rows.shape, I32),
+            pltpu.VMEM(leaf_rows.shape, I32),
+            pltpu.SemaphoreType.DMA((4,)),
+        ),
+    )(core, sep_rhs, sep_update, sep_rows, leaf_rows)
     arrived = swapped(sent)
 
     rhs, spread, select, listed, fits = kernel_call(
@@ -397,7 +426,7 @@
         2 * held * n_sep * chips * SLOTS,
         MIB,
         (0,),
-    )(me, sep_rows, sep_rhs, sep_update, leaf_rows, arrived)
+    )(chip, kept, arrived)
 
     mail = array(chips, SLOTS + LIST, wide)
     blocks = kernel_call(select_body, mail, SLOTS * lines_here * wide, MIB, limit=4)(
@@ -410,7 +439,9 @@
     def all_rows(blocks, lines, listed, sep_rows):
         full = array(chips, lines_here + LIST, wide)
         full = kernel_call(all_lines_body, full, 1024, 2 * MIB)(lines, listed)
-        return kernel_call(functools.partial(all_rows_body, sizes), mail, 1024, 2 * MIB)(sep_rows, to_all(full, XY))
+        return kernel_call(
+            functools.partial(all_rows_body, sizes), mail, 1024, 2 * MIB
+        )(sep_rows, to_all(full, XY))
 
     root_rows = lax.cond(fits[0] == 1, few_rows, all_rows, blocks, lines, listed, sep_rows)
 
@@ -420,12 +451,10 @@
         2 * held * wide * (chips * SLOTS + sep),
         6 * MIB,
         in_hbm=(3, 4),
-        out_hbm=(0,),
         scratch=(
             pltpu.VMEM(sep_inv_cols.shape, BF16),
             pltpu.VMEM(sep_inv_cols.shape, BF16),
-            pltpu.VMEM((chips, wide, sep // chips), BF16),
-            pltpu.SemaphoreType.DMA((2 + chips,)),
+            pltpu.SemaphoreType.DMA((2,)),
         ),
     )(rhs, spread, root_rows, sep_inv_cols, other_inverse)
     terms = to_all(terms, XY)
@@ -434,7 +463,7 @@
         functools.partial(leaf_plan_body, sizes, sep, held),
         (
             array(chips, SLOTS, held + lines_here),
-            array(cores * n_leaf, 1, dtype=I32),
+            array(1, cores * n_leaf, dtype=I32),
             flag,
         ),
         chips * 2**26,
@@ -444,7 +473,7 @@
             pltpu.VMEM((chips, cores * n_leaf), I32),
             pltpu.VMEM((chips, cores * n_leaf), I32),
         ),
-    )(me, root_rows)
+    )(chip, root_rows)
     mail = array(chips, SLOTS, wide)
     value, blocks = kernel_call(
         sum_body, (array(held, wide), mail), 2 * chips * SLOTS * wide * (held + lines_here), 2 * MIB
@@ -456,17 +485,27 @@
     def all_ancestors(blocks, value, lines, listed):
         table = jnp.concatenate([value, lines], axis=0)
         table = to_all(jnp.broadcast_to(table, (chips, *table.shape)), XY)
-        return kernel_call(functools.partial(all_ancestors_body, sizes, sep, held), mail, 1024, 2 * MIB)(listed, table)
+        return kernel_call(
+            functools.partial(all_ancestors_body, sizes, sep, held), mail, 1024, 2 * MIB
+        )(listed, table)
 
     ancestors = lax.cond(fits[0] == 1, few_ancestors, all_ancestors, blocks, value, lines, listed)
 
-    own_rows, sent = kernel_call(
+    own_rows, sent, leaf_rhs, leaf_update = kernel_call(
         ancestors_body,
-        (array(n_leaf, wide), array(n_leaf + own_sep, wide)),
+        (
+            array(n_leaf, wide),
+            array(n_leaf + own_sep, wide),
+            array(*leaf_rhs.shape),
+            array(*leaf_update.shape),
+        ),
         2 * cores * n_leaf * wide * chips * SLOTS,
         MIB,
         (0,),
-    )(me, place, ancestors, value)
+        16,
+        in_hbm=(4, 5),
+        scratch=(pltpu.SemaphoreType.DMA((2,)),),
+    )(core, place, ancestors, value, leaf_rhs, leaf_update)
     arrived = swapped(sent)
     leaf_out, sep_out = kernel_call(
         leaf_body,
@@ -476,7 +515,7 @@
         (0, 1),
         out_hbm=(0,),
         scratch=(pltpu.VMEM(leaf_rhs.shape, BF16), pltpu.SemaphoreType.DMA((4,))),
-    )(me, leaf_cols, own_rows, arrived, value, leaf_rhs, leaf_update, leaf_inv)
+    )(core, leaf_cols, own_rows, arrived, value, leaf_rhs, leaf_update, leaf_inv)
     return (sep_out, leaf_out)
 
 

time: 95.1 us -> 94.7 us (level)
  waiting for transfers between devices: 12 us -> 16.2 us
  local copies, waits for them, and re-layouts: 5.54 us -> 1.62 us
    all_to_all x2, waiting for transfers between devices: 10.6 us -> 14.6 us  [to_all(): return lax.all_to_all(blocks, axes, 0, 0, tiled=True)]
    unnamed x22 -> x12, local copies, waits for them, and re-layouts: 5.54 us -> 1.62 us
where the time goes in v5:
time: 94.7 us; the launch traced here: 94.1 us
  starting transfers between devices  29 us (31%)
  blocking collectives  28.1 us (30%)
  Pallas kernels  16.4 us (17%)
  waiting for transfers between devices  16.2 us (17%)
  between operations  2.7 us (3%)
  local copies, waits for them, and re-layouts  1.62 us (2%)
    all_to_all x2, blocking collectives, to_all(): return lax.all_to_all(blocks, axes, 0, 0, tiled=True)  28.1 us
    pallas_call x9, Pallas kernels, call(): pl.pallas_call(body, out_shape=outs, in_specs=specs, out_specs=jax.tree.u...  16.4 us
    ppermute x3, starting transfers between devices, swapped(): return lax.ppermute(value, CORE, [(0, 1), (1, 0)])  15.3 us
    all_to_all x2, waiting for transfers between devices, to_all(): return lax.all_to_all(blocks, axes, 0, 0, tiled=True)  14.6 us
    all_to_all x2, starting transfers between devices, to_all(): return lax.all_to_all(blocks, axes, 0, 0, tiled=True)  13.7 us
  transfers between devices with their start and end apart: 5, of which 4 were waited for; matrix products, arithmetic and copies ran while one was open for 0% of the time, Pallas kernels for 10%

profile of v5, /device:TPU:1, one launch (start us, length us, event | category | flops | bytes accessed | tf_op | source)
XLA Modules:
  0.0 94.1 jit_solution(11466921085623432173)
XLA Ops:
  0.6 8.8 %collective-permute-start.1 = (bf16[128,4096]{1,0:T(8,128)(2,1)}, bf16[128,4096]{1,0:T(8,128)(2,1)}, u32[]{:S(2)}, u32[]{:S(2)}) collective-permute-start(bf16[128,4096]{1,0:T(8,128)(2,1)} %own_inverse_at.1), channel_id=1, source_target_pairs={{0,1},{1,0},{2,3},{3,2},{4,5},{5,4},{6,7},{7,6},{8,9},{9,8},{10,11... | collective-permute-start | bytes 3145736 | tf_op jit(solution)/shard_map/ppermute | solution.py:25
  9.4 0.7 copy-done.4
  10.1 0.6 shard_map.115
  10.7 10.0 %all-to-all-start.4 = ((bf16[32,8,128]{2,1,0:T(8,128)(2,1)}), bf16[32,8,128]{2,1,0:T(8,128)(2,1)S(1)}, u32[]{:S(2)}, u32[]{:S(2)}) async-start(bf16[32,8,128]{2,1,0:T(8,128)(2,1)} %shard_map.115), calls=%async_computation.4 | async-start | bytes 131072 | tf_op jit(solution)/shard_map/all_to_all | solution.py:21
  20.7 1.7 %shard_map.113 = (bf16[136,640]{1,0:T(8,128)(2,1)}, bf16[136,640]{1,0:T(8,128)(2,1)}) custom-call(s32[1]{0:T(128)} %bitcast.core, bf16[128,256]{1,0:T(8,128)(2,1)} %rhs_at.2, bf16[128,512]{1,0:T(8,128)(2,1)} %update_at.2, s32[1,512]{1,0:T(1,128)} %rows_at.1, s32[1,256]{1,0:T(1,128)} %leaf_rows_at.1), custom_call_target="tpu_custom_call" | custom-call | flops 128 | bytes 1048576 | tf_op jit(solution)/shard_map/pallas_call | solution.py:57
  22.5 2.1 %collective-permute-start = (bf16[136,640]{1,0:T(8,128)(2,1)}, bf16[136,640]{1,0:T(8,128)(2,1)S(1)}, u32[]{:S(2)}, u32[]{:S(2)}) collective-permute-start(bf16[136,640]{1,0:T(8,128)(2,1)} %get-tuple-element.47), channel_id=1, source_target_pairs={{0,1},{1,0},{2,3},{3,2},{4,5},{5,4},{6,7},{7,6},{8,9},{9,8},{10,11... | collective-permute-start | bytes 522248 | tf_op jit(solution)/shard_map/ppermute | solution.py:25
  24.6 1.4 %collective-permute-done.arrived = bf16[136,640]{1,0:T(8,128)(2,1)S(1)} collective-permute-done((bf16[136,640]{1,0:T(8,128)(2,1)}, bf16[136,640]{1,0:T(8,128)(2,1)S(1)}, u32[]{:S(2)}, u32[]{:S(2)}) %collective-permute-start) | collective-permute-done | bytes 174112 | tf_op jit(solution)/shard_map/ppermute | solution.py:25
  26.0 0.9 copy-done.5
  26.9 1.0 %shard_map.114 = (bf16[256,128]{1,0:T(8,128)(2,1)S(1)}, bf16[256,1024]{1,0:T(8,128)(2,1)S(1)}, bf16[64,256]{1,0:T(8,128)(2,1)S(1)}, bf16[8,128]{1,0:T(8,128)(2,1)S(1)}, s32[1]{0:T(128)}) custom-call(s32[1]{0:T(128)} %bitcast.1.chip_at, bf16[136,640]{1,0:T(8,128)(2,1)S(1)} %copy-done.5, bf16[136,640]{1,0:T(8,128)(2,1)S(1)} %collective-permute-done.arrived), custom_call_target="tpu_custom_call" | custom-call | flops 268435456 | bytes 1048576 | tf_op jit(solution)/shard_map/pallas_call | solution.py:57
  28.6 5.8 %all-to-all-done.4 = bf16[32,8,128]{2,1,0:T(8,128)(2,1)S(1)} async-done(((bf16[32,8,128]{2,1,0:T(8,128)(2,1)}), bf16[32,8,128]{2,1,0:T(8,128)(2,1)S(1)}, u32[]{:S(2)}, u32[]{:S(2)}) %all-to-all-start.4) | async-done | bytes 65568 | tf_op jit(solution)/shard_map/all_to_all | solution.py:21
  34.5 0.1 shard_map.116
  34.6 15.3 %conditional.2 = (bf16[16,72,128]{2,1,0:T(8,128)(2,1)S(1)}) conditional(s32[]{:T(128)} %bitcast.2, (bf16[256,128]{1,0:T(8,128)(2,1)S(1)}, bf16[8,128]{1,0:T(8,128)(2,1)S(1)}, s32[1,512]{1,0:T(1,128)}) %tuple.27, bf16[16,72,128]{2,1,0:T(8,128)(2,1)S(1)} %shard_map.116), branch_computations={%region_0.0_spmd, %region_1.0_spmd} | conditional | flops 2048 | bytes 6365220 | solution.py:446
  34.7 15.2 %all_to_all.27 = bf16[16,72,128]{2,1,0:T(8,128)(2,1)S(1)} all-to-all(bf16[16,72,128]{2,1,0:T(8,128)(2,1)S(1)} %param.1), channel_id=1, replica_groups=mesh['grp'=16,'x_1'=2,'x_0'=2,'y_1'=2,'y_0'=2,'core'=2] {'y_0','x_0','y_..., dimensions={0} | all-to-all | bytes 589824 | tf_op jit(solution)/shard_map/cond/branch_1_fun/all_to_all | solution.py:21
  49.9 3.0 %shard_map.118 = bf16[16,128,256]{2,1,0:T(8,128)(2,1)} custom-call(bf16[256,128]{1,0:T(8,128)(2,1)S(1)} %get-tuple-element.53.rhs, bf16[256,1024]{1,0:T(8,128)(2,1)S(1)} %get-tuple-element.54.spread, bf16[16,72,128]{2,1,0:T(8,128)(2,1)S(1)} %get-tuple-element.64.arrived, bf16[128,4096]{1,0:T(8,128)(2,1)S(1)} %copy-done.1, ...), custom_call_target="tpu_custom_call" | custom-call | flops 335544320 | bytes 6291456 | tf_op jit(solution)/shard_map/pallas_call | solution.py:57
  52.9 3.7 %all-to-all-start.5 = ((bf16[16,128,256]{2,1,0:T(8,128)(2,1)}), bf16[16,128,256]{2,1,0:T(8,128)(2,1)S(1)}, u32[]{:S(2)}, u32[]{:S(2)}) async-start(bf16[16,128,256]{2,1,0:T(8,128)(2,1)} %shard_map.118), calls=%async_computation.5 | async-start | bytes 2097152 | tf_op jit(solution)/shard_map/all_to_all | solution.py:21
  56.6 5.4 %shard_map.117 = (bf16[16,64,512]{2,1,0:T(8,128)(2,1)S(1)}, s32[1,512]{1,0:T(1,128)S(1)}, s32[1]{0:T(128)}) custom-call(s32[1]{0:T(128)} %bitcast.1.chip_at, bf16[16,72,128]{2,1,0:T(8,128)(2,1)S(1)} %get-tuple-element.64.arrived), custom_call_target="tpu_custom_call" | custom-call | flops 1073741824 | bytes 2097152 | tf_op jit(solution)/shard_map/pallas_call | solution.py:57
  62.7 8.7 %all-to-all-done.5.terms = bf16[16,128,256]{2,1,0:T(8,128)(2,1)S(1)} async-done(((bf16[16,128,256]{2,1,0:T(8,128)(2,1)}), bf16[16,128,256]{2,1,0:T(8,128)(2,1)S(1)}, u32[]{:S(2)}, u32[]{:S(2)}) %all-to-all-start.5) | async-done | bytes 1048608 | tf_op jit(solution)/shard_map/all_to_all | solution.py:21
  71.4 1.3 %shard_map.119 = (bf16[256,128]{1,0:T(8,128)(2,1)S(1)}, bf16[16,64,128]{2,1,0:T(8,128)(2,1)}) custom-call(bf16[16,128,256]{2,1,0:T(8,128)(2,1)S(1)} %all-to-all-done.5.terms, bf16[16,64,512]{2,1,0:T(8,128)(2,1)S(1)} %get-tuple-element.55.select, bf16[256,128]{1,0:T(8,128)(2,1)S(1)} %bitcast.7), custom_call_target="tpu_custom_call" | custom-call | flops 134217728 | bytes 2097152 | tf_op jit(solution)/shard_map/pallas_call | solution.py:57
  72.7 12.9 %conditional.3 = (bf16[16,64,128]{2,1,0:T(8,128)(2,1)S(1)}) conditional(s32[]{:T(128)} %bitcast.4, (bf16[256,128]{1,0:T(8,128)(2,1)S(1)}, bf16[256,128]{1,0:T(8,128)(2,1)S(1)}, bf16[8,128]{1,0:T(8,128)(2,1)S(1)}) %tuple.28, bf16[16,64,128]{2,1,0:T(8,128)(2,1)} %get-tuple-element.57), branch_computations={%region_2.0_spmd, %region_3.0_spmd} | conditional | flops 263168 | bytes 8781832 | solution.py:492
  72.7 12.9 %all_to_all.29 = bf16[16,64,128]{2,1,0:T(8,128)(2,1)S(1)} all-to-all(bf16[16,64,128]{2,1,0:T(8,128)(2,1)} %param.3), channel_id=1, replica_groups=mesh['grp'=16,'x_1'=2,'x_0'=2,'y_1'=2,'y_0'=2,'core'=2] {'y_0','x_0','y_..., dimensions={0} | all-to-all | bytes 524288 | tf_op jit(solution)/shard_map/cond/branch_1_fun/all_to_all | solution.py:21
  85.6 0.8 shard_map.120
  86.4 4.5 %collective-permute-start.2 = (bf16[384,128]{1,0:T(8,128)(2,1)S(1)}, bf16[384,128]{1,0:T(8,128)(2,1)S(1)}, u32[]{:S(2)}, u32[]{:S(2)}) collective-permute-start(bf16[384,128]{1,0:T(8,128)(2,1)S(1)} %get-tuple-element.59), channel_id=1, source_target_pairs={{0,1},{1,0},{2,3},{3,2},{4,5},{5,4},{6,7},{7,6},{8,9},{9,8},{10,11... | collective-permute-start | bytes 294920 | tf_op jit(solution)/shard_map/ppermute | solution.py:25
  91.5 0.3 collective-permute-done.2.arrived
  91.8 2.3 %shard_map.121 = (bf16[1024,256]{1,0:T(8,128)(2,1)}, bf16[128,256]{1,0:T(8,128)(2,1)}) custom-call(s32[1]{0:T(128)} %bitcast.core, s32[1]{0:T(128)S(6)} %copy.16.cols, bf16[256,128]{1,0:T(8,128)(2,1)S(1)} %get-tuple-element.58.own, bf16[384,128]{1,0:T(8,128)(2,1)S(1)} %collective-permute-done.2.arrived, bf16[256,128]{1,0:T(8,128)(2,1)S(1)} %get-tuple-element.56.value, ...), custom_call_target="tpu_custom_call" | custom-call | flops 671088640 | bytes 4194304 | tf_op jit(solution)/shard_map/pallas_call | solution.py:57
  (11 shorter events, 0.0 us)
Async XLA Ops:
  0.6 49.3 %collective-permute-start.1 = (bf16[128,4096]{1,0:T(8,128)(2,1)}, bf16[128,4096]{1,0:T(8,128)(2,1)}, u32[]{:S(2)}, u32[]{:S(2)}) collective-permute-start(bf16[128,4096]{1,0:T(8,128)(2,1)} %own_inverse_at.1), channel_id=1, source_target_pairs={{0,1},{1,0},{2,3},{3,2},{4,5},{5,4},{6,7},{7,6},{8,9},{9,8},{10,11... | collective-permute-start | bytes 3145736 | tf_op jit(solution)/shard_map/ppermute | solution.py:25
  9.4 0.7 copy-start.4
  10.7 23.8 %all-to-all-start.4 = ((bf16[32,8,128]{2,1,0:T(8,128)(2,1)}), bf16[32,8,128]{2,1,0:T(8,128)(2,1)S(1)}, u32[]{:S(2)}, u32[]{:S(2)}) async-start(bf16[32,8,128]{2,1,0:T(8,128)(2,1)} %shard_map.115), calls=%async_computation.4 | async-start | bytes 131072 | tf_op jit(solution)/shard_map/all_to_all | solution.py:21
  22.5 3.5 %collective-permute-start = (bf16[136,640]{1,0:T(8,128)(2,1)}, bf16[136,640]{1,0:T(8,128)(2,1)S(1)}, u32[]{:S(2)}, u32[]{:S(2)}) collective-permute-start(bf16[136,640]{1,0:T(8,128)(2,1)} %get-tuple-element.47), channel_id=1, source_target_pairs={{0,1},{1,0},{2,3},{3,2},{4,5},{5,4},{6,7},{7,6},{8,9},{9,8},{10,11... | collective-permute-start | bytes 522248 | tf_op jit(solution)/shard_map/ppermute | solution.py:25
  26.0 0.9 copy-start.5
  34.6 15.3 %copy-start.1 = (bf16[128,4096]{1,0:T(8,128)(2,1)S(1)}, bf16[128,4096]{1,0:T(8,128)(2,1)}, u32[]{:S(2)}) copy-start(bf16[128,4096]{1,0:T(8,128)(2,1)} %own_inverse_at.1) | copy-start | bytes 3145732
  52.9 18.5 %all-to-all-start.5 = ((bf16[16,128,256]{2,1,0:T(8,128)(2,1)}), bf16[16,128,256]{2,1,0:T(8,128)(2,1)S(1)}, u32[]{:S(2)}, u32[]{:S(2)}) async-start(bf16[16,128,256]{2,1,0:T(8,128)(2,1)} %shard_map.118), calls=%async_computation.5 | async-start | bytes 2097152 | tf_op jit(solution)/shard_map/all_to_all | solution.py:21
  72.7 12.9 %copy-start.2 = (bf16[1024,256]{1,0:T(8,128)(2,1)S(1)}, bf16[1024,256]{1,0:T(8,128)(2,1)}, u32[]{:S(2)}) copy-start(bf16[1024,256]{1,0:T(8,128)(2,1)} %rhs_at.3) | copy-start | bytes 1572868
  72.7 12.9 %copy-start.3 = (bf16[1024,256]{1,0:T(8,128)(2,1)S(1)}, bf16[1024,256]{1,0:T(8,128)(2,1)}, u32[]{:S(2)}) copy-start(bf16[1024,256]{1,0:T(8,128)(2,1)} %update_at.3) | copy-start | bytes 1572868
  72.7 19.1 %copy-start = (bf16[1024,1024]{1,0:T(8,128)(2,1)S(1)}, bf16[1024,1024]{1,0:T(8,128)(2,1)}, u32[]{:S(2)}) copy-start(bf16[1024,1024]{1,0:T(8,128)(2,1)} %inverse.1) | copy-start | bytes 6291460
  86.4 5.4 %collective-permute-start.2 = (bf16[384,128]{1,0:T(8,128)(2,1)S(1)}, bf16[384,128]{1,0:T(8,128)(2,1)S(1)}, u32[]{:S(2)}, u32[]{:S(2)}) collective-permute-start(bf16[384,128]{1,0:T(8,128)(2,1)S(1)} %get-tuple-element.59), channel_id=1, source_target_pairs={{0,1},{1,0},{2,3},{3,2},{4,5},{5,4},{6,7},{7,6},{8,9},{9,8},{10,11... | collective-permute-start | bytes 294920 | tf_op jit(solution)/shard_map/ppermute | solution.py:25

commit v6 on v5

--- a/solution.py
+++ b/solution.py
@@ -9,7 +9,8 @@
 from jax.sharding import PartitionSpec as P
 
 ALL = ("grp", "x_1", "x_0", "y_1", "y_0", "core")
-XY = ("y_0", "x_0", "y_1", "x_1")
+XY = ("x_1", "x_0", "y_1", "y_0")
+MIXED = ("y_0", "x_0", "y_1", "x_1")
 SLOTS, LIST = 64, 8
 BASE = 64
 CORE = "core"
@@ -92,14 +93,14 @@
 def root_owner(rows, own, cores, devices, groups):
     device = (rows >> log2(own)) & (devices - 1)
     group = rows >> log2(own * devices)
-    line = ((device & (cores - 1)) << log2(groups)) + group
-    return spot(device >> log2(cores)), (line << log2(own)) + (rows & (own - 1))
+    line = (group << log2(cores)) + (device & (cores - 1))
+    return device >> log2(cores), (line << log2(own)) + (rows & (own - 1))
 
 
 def ancestor_owner(sizes, sep, held, rows):
     chip, line = root_owner(rows - sep, *sizes)
     here = rows < sep
-    return jnp.where(here, spot(rows >> log2(held)), chip), jnp.where(here, rows & (held - 1), held + line)
+    return jnp.where(here, rows >> log2(held), chip), jnp.where(here, rows & (held - 1), held + line)
 
 
 def before(size):
@@ -144,10 +145,9 @@
 def fan_body(root, out):
     half = root.shape[1] // 2
     low, high = root[:, :half], root[:, half:]
-    groups = out.shape[0] // 2
-    for i in range(groups):
+    for i in range(0, out.shape[0], 2):
         out[i] = low
-        out[groups + i] = high
+        out[i + 1] = high
 
 
 def pack_body(
@@ -392,7 +392,7 @@
     blocks = kernel_call(fan_body, array(groups * cores, own_root, wide), 1024, MIB, limit=4)(
         root_solution
     )
-    lines = to_all(blocks, (CORE, "grp")).reshape(lines_here, wide)
+    lines = to_all(blocks, ("grp", CORE)).reshape(lines_here, wide)
 
     other_inverse = swapped(sep_inv_cols)
     assert n_sep == 2 * n_leaf
@@ -457,7 +457,7 @@
             pltpu.SemaphoreType.DMA((2,)),
         ),
     )(rhs, spread, root_rows, sep_inv_cols, other_inverse)
-    terms = to_all(terms, XY)
+    terms = to_all(terms, MIXED)
 
     select, place, fits = kernel_call(
         functools.partial(leaf_plan_body, sizes, sep, held),

time: 94.7 us -> 92.5 us (0.977)
  waiting for transfers between devices: 16.2 us -> 14.1 us
  starting transfers between devices: 29 us -> 30.9 us
  blocking collectives: 28.1 us -> 26.3 us
    all_to_all x2, waiting for transfers between devices: 14.6 us -> 12.5 us  [to_all(): return lax.all_to_all(blocks, axes, 0, 0, tiled=True)]
    all_to_all x2, blocking collectives: 28.1 us -> 26.3 us  [to_all(): return lax.all_to_all(blocks, axes, 0, 0, tiled=True)]
    ppermute x3, starting transfers between devices: 15.3 us -> 17.2 us  [swapped(): return lax.ppermute(value, CORE, [(0, 1), (1, 0)])]
where the time goes in v6:
time: 92.5 us; the launch traced here: 92 us
  starting transfers between devices  30.9 us (33%)
  blocking collectives  26.3 us (28%)
  Pallas kernels  16.4 us (18%)
  waiting for transfers between devices  14.1 us (15%)
  between operations  2.7 us (3%)
  local copies, waits for them, and re-layouts  1.62 us (2%)
    all_to_all x2, blocking collectives, to_all(): return lax.all_to_all(blocks, axes, 0, 0, tiled=True)  26.3 us
    ppermute x3, starting transfers between devices, swapped(): return lax.ppermute(value, CORE, [(0, 1), (1, 0)])  17.2 us
    pallas_call x9, Pallas kernels, call(): pl.pallas_call(body, out_shape=outs, in_specs=specs, out_specs=jax.tree.u...  16.4 us
    all_to_all x2, starting transfers between devices, to_all(): return lax.all_to_all(blocks, axes, 0, 0, tiled=True)  13.7 us
    all_to_all x2, waiting for transfers between devices, to_all(): return lax.all_to_all(blocks, axes, 0, 0, tiled=True)  12.5 us
  transfers between devices with their start and end apart: 5, of which 4 were waited for; matrix products, arithmetic and copies ran while one was open for 0% of the time, Pallas kernels for 10%

profile of v6, /device:TPU:1, one launch (start us, length us, event | category | flops | bytes accessed | tf_op | source)
XLA Modules:
  0.0 92.0 jit_solution(3632121439913808715)
XLA Ops:
  0.6 8.8 %collective-permute-start.1 = (bf16[128,4096]{1,0:T(8,128)(2,1)}, bf16[128,4096]{1,0:T(8,128)(2,1)}, u32[]{:S(2)}, u32[]{:S(2)}) collective-permute-start(bf16[128,4096]{1,0:T(8,128)(2,1)} %own_inverse_at.1), channel_id=1, source_target_pairs={{0,1},{1,0},{2,3},{3,2},{4,5},{5,4},{6,7},{7,6},{8,9},{9,8},{10,11... | collective-permute-start | bytes 3145736 | tf_op jit(solution)/shard_map/ppermute | solution.py:26
  9.4 0.7 copy-done.4
  10.1 0.6 shard_map.115
  10.7 10.0 %all-to-all-start.4 = ((bf16[32,8,128]{2,1,0:T(8,128)(2,1)}), bf16[32,8,128]{2,1,0:T(8,128)(2,1)S(1)}, u32[]{:S(2)}, u32[]{:S(2)}) async-start(bf16[32,8,128]{2,1,0:T(8,128)(2,1)} %shard_map.115), calls=%async_computation.4 | async-start | bytes 131072 | tf_op jit(solution)/shard_map/all_to_all | solution.py:22
  20.7 1.7 %shard_map.113 = (bf16[136,640]{1,0:T(8,128)(2,1)}, bf16[136,640]{1,0:T(8,128)(2,1)}) custom-call(s32[1]{0:T(128)} %bitcast.core, bf16[128,256]{1,0:T(8,128)(2,1)} %rhs_at.2, bf16[128,512]{1,0:T(8,128)(2,1)} %update_at.2, s32[1,512]{1,0:T(1,128)} %rows_at.1, s32[1,256]{1,0:T(1,128)} %leaf_rows_at.1), custom_call_target="tpu_custom_call" | custom-call | flops 128 | bytes 1048576 | tf_op jit(solution)/shard_map/pallas_call | solution.py:58
  22.5 2.1 %collective-permute-start = (bf16[136,640]{1,0:T(8,128)(2,1)}, bf16[136,640]{1,0:T(8,128)(2,1)S(1)}, u32[]{:S(2)}, u32[]{:S(2)}) collective-permute-start(bf16[136,640]{1,0:T(8,128)(2,1)} %get-tuple-element.47), channel_id=1, source_target_pairs={{0,1},{1,0},{2,3},{3,2},{4,5},{5,4},{6,7},{7,6},{8,9},{9,8},{10,11... | collective-permute-start | bytes 522248 | tf_op jit(solution)/shard_map/ppermute | solution.py:26
  24.6 1.4 %collective-permute-done.arrived = bf16[136,640]{1,0:T(8,128)(2,1)S(1)} collective-permute-done((bf16[136,640]{1,0:T(8,128)(2,1)}, bf16[136,640]{1,0:T(8,128)(2,1)S(1)}, u32[]{:S(2)}, u32[]{:S(2)}) %collective-permute-start) | collective-permute-done | bytes 174112 | tf_op jit(solution)/shard_map/ppermute | solution.py:26
  26.0 0.9 copy-done.5
  26.9 1.0 %shard_map.114 = (bf16[256,128]{1,0:T(8,128)(2,1)S(1)}, bf16[256,1024]{1,0:T(8,128)(2,1)S(1)}, bf16[64,256]{1,0:T(8,128)(2,1)S(1)}, bf16[8,128]{1,0:T(8,128)(2,1)S(1)}, s32[1]{0:T(128)}) custom-call(s32[1]{0:T(128)} %bitcast.1.chip_at, bf16[136,640]{1,0:T(8,128)(2,1)S(1)} %copy-done.5, bf16[136,640]{1,0:T(8,128)(2,1)S(1)} %collective-permute-done.arrived), custom_call_target="tpu_custom_call" | custom-call | flops 268435456 | bytes 1048576 | tf_op jit(solution)/shard_map/pallas_call | solution.py:58
  28.6 5.1 %all-to-all-done.4 = bf16[32,8,128]{2,1,0:T(8,128)(2,1)S(1)} async-done(((bf16[32,8,128]{2,1,0:T(8,128)(2,1)}), bf16[32,8,128]{2,1,0:T(8,128)(2,1)S(1)}, u32[]{:S(2)}, u32[]{:S(2)}) %all-to-all-start.4) | async-done | bytes 65568 | tf_op jit(solution)/shard_map/all_to_all | solution.py:22
  33.7 0.1 shard_map.116
  33.9 14.2 %conditional.2 = (bf16[16,72,128]{2,1,0:T(8,128)(2,1)S(1)}) conditional(s32[]{:T(128)} %bitcast.2, (bf16[256,128]{1,0:T(8,128)(2,1)S(1)}, bf16[8,128]{1,0:T(8,128)(2,1)S(1)}, s32[1,512]{1,0:T(1,128)}) %tuple.27, bf16[16,72,128]{2,1,0:T(8,128)(2,1)S(1)} %shard_map.116), branch_computations={%region_0.0_spmd, %region_1.0_spmd} | conditional | flops 2048 | bytes 6365220 | solution.py:446
  33.9 14.2 %all_to_all.27 = bf16[16,72,128]{2,1,0:T(8,128)(2,1)S(1)} all-to-all(bf16[16,72,128]{2,1,0:T(8,128)(2,1)S(1)} %param.1), channel_id=1, replica_groups=mesh['grp'=16,'x_1'=2,'x_0'=2,'y_1'=2,'y_0'=2,'core'=2] {'x_1','x_0','y_..., dimensions={0} | all-to-all | bytes 589824 | tf_op jit(solution)/shard_map/cond/branch_1_fun/all_to_all | solution.py:22
  48.2 3.0 %shard_map.118 = bf16[16,128,256]{2,1,0:T(8,128)(2,1)} custom-call(bf16[256,128]{1,0:T(8,128)(2,1)S(1)} %get-tuple-element.53.rhs, bf16[256,1024]{1,0:T(8,128)(2,1)S(1)} %get-tuple-element.54.spread, bf16[16,72,128]{2,1,0:T(8,128)(2,1)S(1)} %get-tuple-element.64.arrived, bf16[128,4096]{1,0:T(8,128)(2,1)S(1)} %copy-done.1, ...), custom_call_target="tpu_custom_call" | custom-call | flops 335544320 | bytes 6291456 | tf_op jit(solution)/shard_map/pallas_call | solution.py:58
  51.2 3.7 %all-to-all-start.5 = ((bf16[16,128,256]{2,1,0:T(8,128)(2,1)}), bf16[16,128,256]{2,1,0:T(8,128)(2,1)S(1)}, u32[]{:S(2)}, u32[]{:S(2)}) async-start(bf16[16,128,256]{2,1,0:T(8,128)(2,1)} %shard_map.118), calls=%async_computation.5 | async-start | bytes 2097152 | tf_op jit(solution)/shard_map/all_to_all | solution.py:22
  54.9 5.4 %shard_map.117 = (bf16[16,64,512]{2,1,0:T(8,128)(2,1)S(1)}, s32[1,512]{1,0:T(1,128)S(1)}, s32[1]{0:T(128)}) custom-call(s32[1]{0:T(128)} %bitcast.1.chip_at, bf16[16,72,128]{2,1,0:T(8,128)(2,1)S(1)} %get-tuple-element.64.arrived), custom_call_target="tpu_custom_call" | custom-call | flops 1073741824 | bytes 2097152 | tf_op jit(solution)/shard_map/pallas_call | solution.py:58
  60.9 7.3 %all-to-all-done.5.terms = bf16[16,128,256]{2,1,0:T(8,128)(2,1)S(1)} async-done(((bf16[16,128,256]{2,1,0:T(8,128)(2,1)}), bf16[16,128,256]{2,1,0:T(8,128)(2,1)S(1)}, u32[]{:S(2)}, u32[]{:S(2)}) %all-to-all-start.5) | async-done | bytes 1048608 | tf_op jit(solution)/shard_map/all_to_all | solution.py:22
  68.3 1.3 %shard_map.119 = (bf16[256,128]{1,0:T(8,128)(2,1)S(1)}, bf16[16,64,128]{2,1,0:T(8,128)(2,1)}) custom-call(bf16[16,128,256]{2,1,0:T(8,128)(2,1)S(1)} %all-to-all-done.5.terms, bf16[16,64,512]{2,1,0:T(8,128)(2,1)S(1)} %get-tuple-element.55.select, bf16[256,128]{1,0:T(8,128)(2,1)S(1)} %bitcast.7), custom_call_target="tpu_custom_call" | custom-call | flops 134217728 | bytes 2097152 | tf_op jit(solution)/shard_map/pallas_call | solution.py:58
  69.6 12.1 %conditional.3 = (bf16[16,64,128]{2,1,0:T(8,128)(2,1)S(1)}) conditional(s32[]{:T(128)} %bitcast.4, (bf16[256,128]{1,0:T(8,128)(2,1)S(1)}, bf16[256,128]{1,0:T(8,128)(2,1)S(1)}, bf16[8,128]{1,0:T(8,128)(2,1)S(1)}) %tuple.28, bf16[16,64,128]{2,1,0:T(8,128)(2,1)} %get-tuple-element.57), branch_computations={%region_2.0_spmd, %region_3.0_spmd} | conditional | flops 263168 | bytes 8781832 | solution.py:492
  69.6 12.1 %all_to_all.29 = bf16[16,64,128]{2,1,0:T(8,128)(2,1)S(1)} all-to-all(bf16[16,64,128]{2,1,0:T(8,128)(2,1)} %param.3), channel_id=1, replica_groups=mesh['grp'=16,'x_1'=2,'x_0'=2,'y_1'=2,'y_0'=2,'core'=2] {'x_1','x_0','y_..., dimensions={0} | all-to-all | bytes 524288 | tf_op jit(solution)/shard_map/cond/branch_1_fun/all_to_all | solution.py:22
  81.7 0.8 shard_map.120
  82.5 6.3 %collective-permute-start.2 = (bf16[384,128]{1,0:T(8,128)(2,1)S(1)}, bf16[384,128]{1,0:T(8,128)(2,1)S(1)}, u32[]{:S(2)}, u32[]{:S(2)}) collective-permute-start(bf16[384,128]{1,0:T(8,128)(2,1)S(1)} %get-tuple-element.59), channel_id=1, source_target_pairs={{0,1},{1,0},{2,3},{3,2},{4,5},{5,4},{6,7},{7,6},{8,9},{9,8},{10,11... | collective-permute-start | bytes 294920 | tf_op jit(solution)/shard_map/ppermute | solution.py:26
  89.4 0.3 collective-permute-done.2.arrived
  89.7 2.3 %shard_map.121 = (bf16[1024,256]{1,0:T(8,128)(2,1)}, bf16[128,256]{1,0:T(8,128)(2,1)}) custom-call(s32[1]{0:T(128)} %bitcast.core, s32[1]{0:T(128)S(6)} %copy.16.cols, bf16[256,128]{1,0:T(8,128)(2,1)S(1)} %get-tuple-element.58.own, bf16[384,128]{1,0:T(8,128)(2,1)S(1)} %collective-permute-done.2.arrived, bf16[256,128]{1,0:T(8,128)(2,1)S(1)} %get-tuple-element.56.value, ...), custom_call_target="tpu_custom_call" | custom-call | flops 671088640 | bytes 4194304 | tf_op jit(solution)/shard_map/pallas_call | solution.py:58
  (11 shorter events, 0.0 us)
Async XLA Ops:
  0.6 47.5 %collective-permute-start.1 = (bf16[128,4096]{1,0:T(8,128)(2,1)}, bf16[128,4096]{1,0:T(8,128)(2,1)}, u32[]{:S(2)}, u32[]{:S(2)}) collective-permute-start(bf16[128,4096]{1,0:T(8,128)(2,1)} %own_inverse_at.1), channel_id=1, source_target_pairs={{0,1},{1,0},{2,3},{3,2},{4,5},{5,4},{6,7},{7,6},{8,9},{9,8},{10,11... | collective-permute-start | bytes 3145736 | tf_op jit(solution)/shard_map/ppermute | solution.py:26
  9.4 0.7 copy-start.4
  10.7 23.0 %all-to-all-start.4 = ((bf16[32,8,128]{2,1,0:T(8,128)(2,1)}), bf16[32,8,128]{2,1,0:T(8,128)(2,1)S(1)}, u32[]{:S(2)}, u32[]{:S(2)}) async-start(bf16[32,8,128]{2,1,0:T(8,128)(2,1)} %shard_map.115), calls=%async_computation.4 | async-start | bytes 131072 | tf_op jit(solution)/shard_map/all_to_all | solution.py:22
  22.5 3.5 %collective-permute-start = (bf16[136,640]{1,0:T(8,128)(2,1)}, bf16[136,640]{1,0:T(8,128)(2,1)S(1)}, u32[]{:S(2)}, u32[]{:S(2)}) collective-permute-start(bf16[136,640]{1,0:T(8,128)(2,1)} %get-tuple-element.47), channel_id=1, source_target_pairs={{0,1},{1,0},{2,3},{3,2},{4,5},{5,4},{6,7},{7,6},{8,9},{9,8},{10,11... | collective-permute-start | bytes 522248 | tf_op jit(solution)/shard_map/ppermute | solution.py:26
  26.0 0.9 %copy-start.5 = (bf16[136,640]{1,0:T(8,128)(2,1)S(1)}, bf16[136,640]{1,0:T(8,128)(2,1)}, u32[]{:S(2)}) copy-start(bf16[136,640]{1,0:T(8,128)(2,1)} %get-tuple-element.46.kept) | copy-start | bytes 522244
  33.9 14.2 %copy-start.1 = (bf16[128,4096]{1,0:T(8,128)(2,1)S(1)}, bf16[128,4096]{1,0:T(8,128)(2,1)}, u32[]{:S(2)}) copy-start(bf16[128,4096]{1,0:T(8,128)(2,1)} %own_inverse_at.1) | copy-start | bytes 3145732
  51.2 17.1 %all-to-all-start.5 = ((bf16[16,128,256]{2,1,0:T(8,128)(2,1)}), bf16[16,128,256]{2,1,0:T(8,128)(2,1)S(1)}, u32[]{:S(2)}, u32[]{:S(2)}) async-start(bf16[16,128,256]{2,1,0:T(8,128)(2,1)} %shard_map.118), calls=%async_computation.5 | async-start | bytes 2097152 | tf_op jit(solution)/shard_map/all_to_all | solution.py:22
  69.6 12.1 %copy-start.2 = (bf16[1024,256]{1,0:T(8,128)(2,1)S(1)}, bf16[1024,256]{1,0:T(8,128)(2,1)}, u32[]{:S(2)}) copy-start(bf16[1024,256]{1,0:T(8,128)(2,1)} %rhs_at.3) | copy-start | bytes 1572868
  69.6 12.1 %copy-start.3 = (bf16[1024,256]{1,0:T(8,128)(2,1)S(1)}, bf16[1024,256]{1,0:T(8,128)(2,1)}, u32[]{:S(2)}) copy-start(bf16[1024,256]{1,0:T(8,128)(2,1)} %update_at.3) | copy-start | bytes 1572868
  69.6 20.1 %copy-start = (bf16[1024,1024]{1,0:T(8,128)(2,1)S(1)}, bf16[1024,1024]{1,0:T(8,128)(2,1)}, u32[]{:S(2)}) copy-start(bf16[1024,1024]{1,0:T(8,128)(2,1)} %inverse.1) | copy-start | bytes 6291460
  82.5 7.2 %collective-permute-start.2 = (bf16[384,128]{1,0:T(8,128)(2,1)S(1)}, bf16[384,128]{1,0:T(8,128)(2,1)S(1)}, u32[]{:S(2)}, u32[]{:S(2)}) collective-permute-start(bf16[384,128]{1,0:T(8,128)(2,1)S(1)} %get-tuple-element.59), channel_id=1, source_target_pairs={{0,1},{1,0},{2,3},{3,2},{4,5},{5,4},{6,7},{7,6},{8,9},{9,8},{10,11... | collective-permute-start | bytes 294920 | tf_op jit(solution)/shard_map/ppermute | solution.py:26
